TPU v7x, 32 devices: a whole 2x2x4 slice. The times are simulated.
32 devices in a mesh: dp: 8 (over y, x, core), tensor: 4 (over z).
Axes of the slice: x: 2, y: 2, z: 4, core: 2. Of those that a mesh axis runs over, the one named last changes fastest.
Arguments:
- layer_input: bfloat16 [12288, 2048], P('dp'), may hold values from -30 to 30
- cotangent: bfloat16 [12288, 2048], P('dp'), may hold values from -6 to 6
- lengths: int32 [24], P('dp'), may hold values from 0 to 512, as said below
- projector: float32 [2048, 6144], P('dp', 'tensor'), may hold values from -0.125 to 0.125
- projector_moments: float32 [2, 2048, 6144], P(None, 'dp', 'tensor'), as said below
- shifts: float32 [8, 768], P('tensor', 'dp'), may hold values from -3 to 3
- shifts_moments: float32 [2, 8, 768], P(None, 'tensor', 'dp'), as said below
- combiner: float32 [2048, 2048], P('tensor', 'dp'), may hold values from -1.5 to 1.5
- combiner_moments: float32 [2, 2048, 2048], P(None, 'tensor', 'dp'), as said below
- expander: float32 [2048, 8192], P('dp', 'tensor'), may hold values from -0.125 to 0.125
- expander_moments: float32 [2, 2048, 8192], P(None, 'dp', 'tensor'), as said below
- offsets: float32 [8, 1024], P('tensor', 'dp'), may hold values from -3 to 3
- offsets_moments: float32 [2, 8, 1024], P(None, 'tensor', 'dp'), as said below
- reducer: float32 [8192, 2048], P('tensor', 'dp'), may hold values from -0.0625 to 0.0625
- reducer_moments: float32 [2, 8192, 2048], P(None, 'tensor', 'dp'), as said below
- vectors: float32 [6, 2048], P(None, ('dp', 'tensor')), may hold values from -2 to 2
- vectors_moments: float32 [2, 6, 2048], P(None, None, ('dp', 'tensor')), as said below
Outputs:
- layer_output: bfloat16 [12288, 2048], P('dp', 'tensor')
- input_gradient: bfloat16 [12288, 2048], P('dp', 'tensor')
- projector_gradient: float32 [2048, 6144], P('dp', 'tensor')
- projector_states: float32 [2, 2048, 6144], P(None, 'dp', 'tensor')
- projector_update: float32 [2048, 6144], P('dp', 'tensor')
- shifts_gradient: float32 [8, 768], P('tensor', 'dp')
- shifts_states: float32 [2, 8, 768], P(None, 'tensor', 'dp')
- shifts_update: float32 [8, 768], P('tensor', 'dp')
- combiner_gradient: float32 [2048, 2048], P('tensor', 'dp')
- combiner_states: float32 [2, 2048, 2048], P(None, 'tensor', 'dp')
- combiner_update: float32 [2048, 2048], P('tensor', 'dp')
- expander_gradient: float32 [2048, 8192], P('dp', 'tensor')
- expander_states: float32 [2, 2048, 8192], P(None, 'dp', 'tensor')
- expander_update: float32 [2048, 8192], P('dp', 'tensor')
- offsets_gradient: float32 [8, 1024], P('tensor', 'dp')
- offsets_states: float32 [2, 8, 1024], P(None, 'tensor', 'dp')
- offsets_update: float32 [8, 1024], P('tensor', 'dp')
- reducer_gradient: float32 [8192, 2048], P('tensor', 'dp')
- reducer_states: float32 [2, 8192, 2048], P(None, 'tensor', 'dp')
- reducer_update: float32 [8192, 2048], P('tensor', 'dp')
- vectors_gradient: float32 [6, 2048], P(None, ('dp', 'tensor'))
- vectors_states: float32 [2, 6, 2048], P(None, None, ('dp', 'tensor'))
- vectors_update: float32 [6, 2048], P(None, ('dp', 'tensor'))
Inputs may be any that keep to these rules, and one draw needn't show every extreme that they name: `lengths`: dp index i holds slots i * 3 to i * 3 + 2; a slot is empty (0) or holds one sequence of 128 to 512 tokens; every index holds at least one sequence, some index has all its slots filled, one of them with 512 tokens, and some index holds exactly one sequence. `projector_moments`: the roots of the second moments (index 1 of the first dimension) are positive. `shifts_moments`: the roots of the second moments are positive. `combiner_moments`: the roots of the second moments are positive. `expander_moments`: the roots of the second moments are positive. `offsets_moments`: the roots of the second moments are positive. `reducer_moments`: the roots of the second moments are positive. `vectors_moments`: the roots of the second moments are positive.
All inputs are finite; a program needn't handle non-finite values.
Results may differ from a plain program's by a relative error of at most 0.014.
The roundings to bfloat16 on the way count: a program that leaves them out, or rounds other values in their place, can miss the bound.
Values may be sent and summed in bfloat16 or wider, within the bound.
A program may use at most 320 MiB of HBM per device.

v0:
```python
import math

import jax
import jax.numpy as jnp
from jax import lax
from jax.sharding import PartitionSpec as P

HD = 256
ROT = 64
SEQ_LEN = 512
STEP = 10


layer_eps = 1e-05
adam_eps = 1e-08
beta_one = 0.9
beta_two = 0.95
learn_rate = 0.02
decay_rate = 0.01
rotary_base = 10000.0


def norm_layer(values, scale_row, shift_row):
    average = jnp.mean(values, axis=-1, keepdims=True)
    centred = values - average
    variance = jnp.mean(centred * centred, axis=-1, keepdims=True)
    return centred * lax.rsqrt(variance + layer_eps) * scale_row + shift_row


def exact_gelu(values):
    return jax.nn.gelu(values, approximate=False)


def rotary_tables():
    half_rot = ROT // 2
    frequency = jnp.exp(
        jnp.arange(half_rot, dtype=jnp.float32) * (-2.0 * math.log(rotary_base) / ROT)
    )
    angles = jnp.arange(SEQ_LEN, dtype=jnp.float32)[:, None] * frequency[None, :]
    return (jnp.cos(angles)[:, None, :], jnp.sin(angles)[:, None, :])


def rotate(values, cos_table, sin_table):
    half_rot = ROT // 2
    leading = values[..., :half_rot]
    trailing = values[..., half_rot:ROT]
    return jnp.concatenate(
        [
            leading * cos_table - trailing * sin_table,
            trailing * cos_table + leading * sin_table,
            values[..., ROT:],
        ],
        axis=-1,
    )


def allowed_mask(length):
    position = jnp.arange(SEQ_LEN)
    return (position[None, :] <= position[:, None]) & (position[None, :] < jnp.maximum(length, 1))


def contract_rows(left, right):
    return lax.dot_general(
        left, right, (((0,), (0,)), ((), ())), preferred_element_type=jnp.float32
    )


def contract_cols(left, right):
    return lax.dot_general(
        left, right, (((1,), (1,)), ((), ())), preferred_element_type=jnp.float32
    )


def masked_scores(query_rows, key_rows, length):
    scores = jnp.einsum(
        "qhd,khd->hqk", query_rows, key_rows, preferred_element_type=jnp.float32
    ) * HD ** (-0.5)
    return jnp.where(allowed_mask(length)[None], scores, -1e30)


def attend_forward(query_rows, key_rows, value_rows, length):
    scores = masked_scores(query_rows, key_rows, length)
    largest = jnp.max(scores, axis=-1, keepdims=True)
    powers = jnp.exp(scores - largest)
    row_total = jnp.sum(powers, axis=-1, keepdims=True)
    weights = (powers / row_total).astype(jnp.bfloat16)
    mixture = jnp.einsum("hqk,khd->qhd", weights, value_rows, preferred_element_type=jnp.float32)
    return (mixture.astype(jnp.bfloat16), (largest + jnp.log(row_total))[..., 0])


def attend_backward(query_rows, key_rows, value_rows, length, summary, incoming):
    scores = masked_scores(query_rows, key_rows, length)
    weights = jnp.exp(scores - summary[..., None])
    pushed = jnp.einsum("qhd,khd->hqk", incoming, value_rows, preferred_element_type=jnp.float32)
    inner_sum = jnp.sum(weights * pushed, axis=-1, keepdims=True)
    dscores = (weights * (pushed - inner_sum)).astype(jnp.bfloat16)
    score_scale = HD ** (-0.5)
    grad_query = (
        jnp.einsum("hqk,khd->qhd", dscores, key_rows, preferred_element_type=jnp.float32)
        * score_scale
    )
    grad_keys = (
        jnp.einsum("hqk,qhd->khd", dscores, query_rows, preferred_element_type=jnp.float32)
        * score_scale
    )
    grad_values = jnp.einsum(
        "hqk,qhd->khd", weights.astype(jnp.bfloat16), incoming, preferred_element_type=jnp.float32
    )
    return (grad_query, grad_keys, grad_values)


def forward_slot(pieces):
    query_rows, key_rows, value_rows, length = pieces
    return attend_forward(query_rows, key_rows, value_rows, length)


def backward_slot(pieces):
    query_rows, key_rows, value_rows, length, summary, incoming = pieces
    return attend_backward(query_rows, key_rows, value_rows, length, summary, incoming)


def adamw(master, moments, gradient):
    first_moment = beta_one * moments[0] + (1.0 - beta_one) * gradient
    root_moment = jnp.sqrt(
        beta_two * moments[1] * moments[1] + (1.0 - beta_two) * gradient * gradient
    )
    first_hat = first_moment / (1.0 - beta_one**STEP)
    root_hat = root_moment / math.sqrt(1.0 - beta_two**STEP)
    update = -learn_rate * (first_hat / (root_hat + adam_eps) + decay_rate * master)
    return (jnp.stack([first_moment, root_moment]), update)


def on_device(
    layer_input,
    cotangent,
    lengths,
    projector,
    projector_moments,
    shifts,
    shifts_moments,
    combiner,
    combiner_moments,
    expander,
    expander_moments,
    offsets,
    offsets_moments,
    reducer,
    reducer_moments,
    vectors,
    vectors_moments,
):
    entry, entry_shift, combine, expand, expand_shift, shrink = (
        lax.all_gather(projector.astype(jnp.bfloat16), "dp", axis=0, tiled=True),
        lax.all_gather(shifts.astype(jnp.bfloat16), "dp", axis=1, tiled=True),
        lax.all_gather(combiner.astype(jnp.bfloat16), "dp", axis=1, tiled=True),
        lax.all_gather(expander.astype(jnp.bfloat16), "dp", axis=0, tiled=True),
        lax.all_gather(offsets.astype(jnp.bfloat16), "dp", axis=1, tiled=True),
        lax.all_gather(reducer.astype(jnp.bfloat16), "dp", axis=1, tiled=True),
    )
    full_vectors = lax.all_gather(
        vectors.astype(jnp.bfloat16), ("dp", "tensor"), axis=1, tiled=True
    ).astype(jnp.float32)
    slot_count = lengths.shape[0]
    row_count = slot_count * SEQ_LEN
    local_heads = entry.shape[1] // (3 * HD)
    cos_table, sin_table = rotary_tables()
    inputs = layer_input.astype(jnp.float32)
    first_norm, first_back = jax.vjp(norm_layer, inputs, full_vectors[0], full_vectors[1])
    normed_one = first_norm.astype(jnp.bfloat16)
    packed = jnp.dot(normed_one, entry, preferred_element_type=jnp.float32) + entry_shift.astype(
        jnp.float32
    ).reshape(-1)
    packed = packed.reshape(slot_count, SEQ_LEN, local_heads, 3, HD)
    query_rows = rotate(packed[:, :, :, 0], cos_table, sin_table).astype(jnp.bfloat16)
    key_rows = rotate(packed[:, :, :, 1], cos_table, sin_table).astype(jnp.bfloat16)
    value_rows = packed[:, :, :, 2].astype(jnp.bfloat16)
    mixture, summary = lax.map(forward_slot, (query_rows, key_rows, value_rows, lengths))
    attended = mixture.reshape(row_count, local_heads * HD)
    second_norm, second_back = jax.vjp(norm_layer, inputs, full_vectors[2], full_vectors[3])
    normed_two = second_norm.astype(jnp.bfloat16)
    hidden = jnp.dot(normed_two, expand, preferred_element_type=jnp.float32) + expand_shift.astype(
        jnp.float32
    ).reshape(-1)
    activated, gelu_back = jax.vjp(exact_gelu, hidden)
    activated = activated.astype(jnp.bfloat16)
    partial_sum = jnp.dot(attended, combine, preferred_element_type=jnp.float32) + jnp.dot(
        activated, shrink, preferred_element_type=jnp.float32
    )
    summed = lax.psum_scatter(
        partial_sum.astype(jnp.bfloat16), "tensor", scatter_dimension=1, tiled=True
    ).astype(jnp.float32)
    own_width = summed.shape[1]
    own_start = lax.axis_index("tensor") * own_width
    own_input = lax.dynamic_slice_in_dim(inputs, own_start, own_width, 1)
    own_bias = lax.dynamic_slice_in_dim(full_vectors[4] + full_vectors[5], own_start, own_width, 0)
    live_rows = (
        (jnp.arange(SEQ_LEN)[None, :] < lengths[:, None]).astype(jnp.float32).reshape(row_count, 1)
    )
    layer_output = (live_rows * (own_input + summed + own_bias)).astype(jnp.bfloat16)
    upstream_float = cotangent.astype(jnp.float32) * live_rows
    upstream = upstream_float.astype(jnp.bfloat16)
    dactivated = contract_cols(upstream, shrink)
    dhidden = gelu_back(dactivated)[0].astype(jnp.bfloat16)
    expand_local = contract_rows(normed_two, dhidden)
    expand_bias_local = jnp.sum(dhidden.astype(jnp.float32), axis=0).reshape(expand_shift.shape)
    shrink_local = contract_rows(activated, upstream)
    dnormed_two = contract_cols(dhidden, expand)
    dattended = contract_cols(upstream, combine).astype(jnp.bfloat16)
    combine_local = contract_rows(attended, upstream)
    incoming = dattended.reshape(slot_count, SEQ_LEN, local_heads, HD)
    grad_query, grad_keys, grad_values = lax.map(
        backward_slot, (query_rows, key_rows, value_rows, lengths, summary, incoming)
    )
    grad_query = rotate(grad_query, cos_table, -sin_table)
    grad_keys = rotate(grad_keys, cos_table, -sin_table)
    dpacked = (
        jnp.stack([grad_query, grad_keys, grad_values], axis=3)
        .reshape(row_count, 3 * local_heads * HD)
        .astype(jnp.bfloat16)
    )
    entry_local = contract_rows(normed_one, dpacked)
    entry_bias_local = jnp.sum(dpacked.astype(jnp.float32), axis=0).reshape(entry_shift.shape)
    dnormed_one = contract_cols(dpacked, entry)
    dinput_one, dscale_one, dshift_one = first_back(dnormed_one)
    dinput_two, dscale_two, dshift_two = second_back(dnormed_two)
    bias_total = jnp.sum(upstream_float, axis=0)
    vector_local = jnp.stack(
        [dscale_one, dshift_one, dscale_two, dshift_two, bias_total, bias_total]
    )
    (
        entry_share,
        entry_bias_share,
        combine_share,
        vector_share,
        expand_share,
        expand_bias_share,
        shrink_share,
    ) = (
        lax.psum_scatter(entry_local, "dp", scatter_dimension=0, tiled=True),
        lax.psum_scatter(entry_bias_local, "dp", scatter_dimension=1, tiled=True),
        lax.psum_scatter(combine_local, "dp", scatter_dimension=1, tiled=True),
        lax.psum_scatter(vector_local, "dp", scatter_dimension=1, tiled=True),
        lax.psum_scatter(expand_local, "dp", scatter_dimension=0, tiled=True),
        lax.psum_scatter(expand_bias_local, "dp", scatter_dimension=1, tiled=True),
        lax.psum_scatter(shrink_local, "dp", scatter_dimension=1, tiled=True),
    )
    input_part, norm_share = (
        lax.psum_scatter(
            (dinput_one + dinput_two).astype(jnp.bfloat16),
            "tensor",
            scatter_dimension=1,
            tiled=True,
        ).astype(jnp.float32),
        lax.psum_scatter(
            vector_share[:4].astype(jnp.bfloat16), "tensor", scatter_dimension=1, tiled=True
        ).astype(jnp.float32),
    )
    own_cot = lax.dynamic_slice_in_dim(upstream_float, own_start, own_width, 1)
    input_gradient = (input_part + own_cot).astype(jnp.bfloat16)
    piece_width = vector_share.shape[1] // lax.axis_size("tensor")
    bias_share = lax.dynamic_slice_in_dim(
        vector_share[4:], lax.axis_index("tensor") * piece_width, piece_width, 1
    )
    vector_gradient = jnp.concatenate([norm_share, bias_share], axis=0)
    projector_states, projector_update = adamw(projector, projector_moments, entry_share)
    shifts_states, shifts_update = adamw(shifts, shifts_moments, entry_bias_share)
    combiner_states, combiner_update = adamw(combiner, combiner_moments, combine_share)
    expander_states, expander_update = adamw(expander, expander_moments, expand_share)
    offsets_states, offsets_update = adamw(offsets, offsets_moments, expand_bias_share)
    reducer_states, reducer_update = adamw(reducer, reducer_moments, shrink_share)
    vectors_states, vectors_update = adamw(vectors, vectors_moments, vector_gradient)
    return (
        layer_output,
        input_gradient,
        entry_share,
        projector_states,
        projector_update,
        entry_bias_share,
        shifts_states,
        shifts_update,
        combine_share,
        combiner_states,
        combiner_update,
        expand_share,
        expander_states,
        expander_update,
        expand_bias_share,
        offsets_states,
        offsets_update,
        shrink_share,
        reducer_states,
        reducer_update,
        vector_gradient,
        vectors_states,
        vectors_update,
    )


def solution(mesh):
    placed = (
        P("dp", None),
        P("dp", None),
        P("dp"),
        P("dp", "tensor"),
        P(None, "dp", "tensor"),
        P("tensor", "dp"),
        P(None, "tensor", "dp"),
        P("tensor", "dp"),
        P(None, "tensor", "dp"),
        P("dp", "tensor"),
        P(None, "dp", "tensor"),
        P("tensor", "dp"),
        P(None, "tensor", "dp"),
        P("tensor", "dp"),
        P(None, "tensor", "dp"),
        P(None, ("dp", "tensor")),
        P(None, None, ("dp", "tensor")),
    )
    return jax.shard_map(
        on_device,
        mesh=mesh,
        in_specs=placed,
        out_specs=(
            P("dp", "tensor"),
            P("dp", "tensor"),
            P("dp", "tensor"),
            P(None, "dp", "tensor"),
            P("dp", "tensor"),
            P("tensor", "dp"),
            P(None, "tensor", "dp"),
            P("tensor", "dp"),
            P("tensor", "dp"),
            P(None, "tensor", "dp"),
            P("tensor", "dp"),
            P("dp", "tensor"),
            P(None, "dp", "tensor"),
            P("dp", "tensor"),
            P("tensor", "dp"),
            P(None, "tensor", "dp"),
            P("tensor", "dp"),
            P("tensor", "dp"),
            P(None, "tensor", "dp"),
            P("tensor", "dp"),
            P(None, ("dp", "tensor")),
            P(None, None, ("dp", "tensor")),
            P(None, ("dp", "tensor")),
        ),
        check_vma=False,
    )
```

profile of v0, /device:TPU:0, one launch (start us, length us, event | category | flops | bytes accessed | tf_op | source)
XLA Modules:
  0.0 1193.5 jit_solution(17004085662014109550)
XLA Ops:
  9.7 2.7 convert_element_type.128
  12.6 10.3 all-gather.1
  23.0 69.1 %all-gather = bf16[32,64,6]{1,2,0:T(8,128)(2,1)S(1)} all-gather(bf16[1,64,6]{1,2,0:T(8,128)(2,1)S(1)} %convert_bitcast_fusion.1), channel_id=1, replica_groups=mesh['dp'=8,'tensor'=4] {'dp','tensor'}, dimensions={0}, use_global_device_ids=true | all-gather | bytes 25344 | tf_op jit(solution)/shard_map/all_gather | solution.py:160
  92.2 9.1 all_gather.26
  101.3 3.7 convert_reduce_fusion.2
  105.0 4.6 multiply_reduce_fusion.5
  112.2 16.0 %convolution_add_fusion = f32[1536,1536]{1,0:T(8,128)} fusion(bf16[2048,1536]{1,0:T(8,128)(2,1)} %all-gather.7.cloned.1.call-done, f32[1536]{0:T(1024)S(1)} %reshape.413, bf16[1536,2048]{1,0:T(8,128)(2,1)} %param.21, f32[2048]{0:T(1024)S(1)} %bitcast.340, f32[2048]{0:T(1024)S(1)} %bitcast.321, f32[1536]{0:T(1024)S(1)} %fusion.64, ...), kind=kOutput, calls=%fused_computation.89 | convolution fusion | flops 9684910080 | bytes 22054912 | tf_op jit(solution)/shard_map/dot_general | solution.py:170
  128.2 15.8 %reshape.403 = f32[3,512,2,3,256]{4,3,2,1,0:T(4,128)} reshape(f32[1536,1536]{1,0:T(8,128)} %convolution_add_fusion) | data formatting | bytes 18874368 | tf_op jit(solution)/shard_map/reshape | solution.py:173
  144.0 7.8 slice.258
  151.8 6.6 copy.186
  158.4 13.8 %fusion.105 = (f32[3,512,2,1,256]{4,3,2,1,0:T(1,128)S(1)}, f32[3,512,2,1,256]{4,3,2,1,0:T(1,128)S(1)}) fusion(f32[3,512,2,3,256]{4,3,2,1,0:T(4,128)} %reshape.403), kind=kLoop, calls=%fused_computation.225 | loop fusion | bytes 12582912 | tf_op jit(solution)/shard_map/slice | solution.py:175
  178.9 4.5 subtract_convert_fusion
  183.5 11.1 pad_maximum_fusion.3
  196.2 23.0 %while.26 = (s32[]{:T(128)}, bf16[3,512,2,256]{3,2,1,0:T(2,128)(2,1)}, f32[3,2,512]{2,1,0:T(2,128)}, bf16[3,512,2,256]{1,3,2,0:T(8,128)(2,1)}, s32[3]{0:T(128)S(...) while((s32[]{:T(128)}, ...), condition=%wide.region_5.6_spmd, body=%wide.region_2.5_spmd.sunk | while | flops 543948288 | bytes 11569293 | solution.py:177
  222.6 8.0 fusion.95
  230.7 48.2 %multiply_convert_fusion.1 = (bf16[1536,2048]{1,0:T(8,128)(2,1)S(1)}, f32[1536,2048]{1,0:T(8,128)}, f32[1536,2048]{1,0:T(8,128)}) fusion(f32[2048]{0:T(1024)S(1)} %bitcast.342, bf16[2048,2048]{1,0:T(8,128)(2,1)} %all-gather.11.cloned.1.call-done, bf16[1536,2048]{1,0:T(8,128)(2,1)} %param.21, f32[2048]{0:T(1024)S(1)} %bitcast.338, f32[2048]{0:T(1024)S(1)} %bitcast.316, ...), kind=kOutput, calls=%fused_computation.70 | convolution fusion | flops 13111394304 | bytes 46174208 | tf_op jit(solution)/shard_map/dot_general | solution.py:181
  281.6 19.6 %fusion.93 = f32[2048,2048]{1,0:T(8,128)} fusion(bf16[1536,2048]{1,0:T(8,128)(2,1)S(1)} %get-tuple-element.368, f32[1536]{0:T(1024)S(1)} %reshape.412, bf16[1536,2048]{1,0:T(8,128)(2,1)} %param.22), kind=kOutput, calls=%fused_computation.220 | convolution fusion | flops 12894339072 | bytes 29366272 | tf_op jit(solution)/shard_map/dot_general | solution.py:63
  302.4 2.9 add_multiply_fusion.3
  305.4 109.2 %reduce-scatter.27.cloned.1.call-done = f32[2048,256]{1,0:T(8,128)} async-done(((f32[2048,2048]{1,0:T(8,128)}), f32[2048,256]{1,0:T(8,128)}) %reduce-scatter.27.cloned.1.call-update) | async-done | bytes 2097168 | tf_op jit(solution)/shard_map/reduce_scatter | solution.py:245
  414.6 6.9 add_multiply_fusion
  421.9 9.6 fusion.86
  432.9 11.6 all-gather.9.cloned.1.call-done
  444.5 8.1 convolution_convert_fusion.1
  452.6 3.8 reshape.405
  456.4 33.5 %while.27 = (s32[]{:T(128)}, f32[3,512,2,256]{1,3,2,0:T(8,128)}, f32[3,512,2,256]{1,3,2,0:T(8,128)}, bf16[3,512,2,256]{1,3,2,0:T(8,128)(2,1)}, bf16[3,512,2,256]...) while((s32[]{:T(128)}, f32[3,512,2,256]{1,3,2,0:T(8,128)}, ...), condition=%wide.region_9.10_spmd, body=%wide.region_7.9_spmd.sunk | while | flops 1347943936 | bytes 36724960 | solution.py:211
  498.1 11.1 copy.175
  509.2 13.0 %convert_element_type.139 = bf16[1536,1536]{1,0:T(8,128)(2,1)} reshape(bf16[3,512,2,3,256]{4,3,2,1,0:T(4,128)(2,1)} %copy.175) | data formatting | bytes 9437184 | tf_op jit(solution)/shard_map/convert_element_type | solution.py:219
  522.2 26.9 %convert_reduce_fusion = (f32[2048]{0:T(1024)S(1)}, bf16[1536,2048]{1,0:T(8,128)(2,1)}) fusion(f32[1536,2048]{1,0:T(8,128)} %get-tuple-element.369, bf16[2048,2048]{1,0:T(8,128)(2,1)} %all-gather.13.cloned.1.call-done, f32[1536]{0:T(1024)S(1)} %reshape.412, bf16[1536,2048]{1,0:T(8,128)(2,1)} %param.22, f32[1536,2048]{1,0:T(8,128)} %get-tuple-element.429, ...), kind=kOutput, calls=%fused_computation.63 | convolution fusion | flops 12947814400 | bytes 46159872 | tf_op jit(solution)/shard_map/dot_general | solution.py:69
  549.1 19.3 %fusion.109 = f32[1536,2048]{1,0:T(8,128)} fusion(bf16[1536,2048]{1,0:T(8,128)(2,1)} %get-tuple-element.432, bf16[2048,2048]{1,0:T(8,128)(2,1)} %all-gather.11.cloned.1.call-done), kind=kOutput, calls=%fused_computation.229 | convolution fusion | flops 12884901888 | bytes 27262976 | tf_op jit(solution)/shard_map/dot_general | solution.py:69
  568.4 22.1 %fusion.103 = (f32[2048]{0:T(1024)S(1)}, f32[1536]{0:T(1024)S(1)}, f32[1536]{0:T(1024)S(1)}, f32[2048]{0:T(1024)S(1)}, f32[1536,2048]{1,0:T(8,128)}) fusion(f32[2048]{0:T(1024)S(1)} %bitcast.322, f32[1536]{0:T(1024)S(1)} %copy-done.23, bf16[1536,2048]{1,0:T(8,128)(2,1)} %param.21, f32[1536,2048]{1,0:T(8,128)} %fusion.109, f32[2048]{0:T(1024)S(1)} %bitcast.317, ...), kind=kOutput, calls=%fused_computation.224 | convolution fusion | flops 9695125504 | bytes 42518528 | tf_op jit(solution)/shard_map/dot_general | solution.py:69
  590.6 14.1 %multiply_reduce_fusion.1 = (f32[2048]{0:T(1024)S(1)}, f32[1536]{0:T(1024)S(1)}, f32[1536]{0:T(1024)S(1)}, f32[2048]{0:T(1024)S(1)}) fusion(f32[1536,2048]{1,0:T(8,128)} %fusion.109, bf16[1536,2048]{1,0:T(8,128)(2,1)} %param.21, f32[1536]{0:T(1024)S(1)} %copy-done.31, f32[1536]{0:T(1024)S(1)} %copy-done.23, f32[1536]{0:T(1024)S(1)} %get-tuple-element.413, ...), kind=kLoop, calls=%fused_computation.61 | loop fusion | flops 59761664 | bytes 31526912 | tf_op jit(solution)/shard_map/transpose(jvp())/reduce_sum | solution.py:27
  607.0 16.7 %fusion.90 = f32[2048,1536]{1,0:T(8,128)} fusion(bf16[1536,1536]{1,0:T(8,128)(2,1)} %convert_element_type.139, bf16[1536,2048]{1,0:T(8,128)(2,1)} %param.21, f32[2048]{0:T(1024)S(1)} %bitcast.341, f32[2048]{0:T(1024)S(1)} %bitcast.324, f32[1536]{0:T(1024)S(1)} %copy-done.31, f32[1536]{0:T(1024)S(1)} %copy-done.23), kind=kOutput, calls=%fused_computation.217 | convolution fusion | flops 9682550784 | bytes 23621632 | tf_op jit(solution)/shard_map/dot_general | solution.py:63
  624.8 14.3 %reduce-scatter.29.cloned.1.call-done = f32[6,256]{1,0:T(8,128)} async-done(((f32[6,2048]{1,0:T(8,128)}), f32[6,256]{1,0:T(8,128)}) %reduce-scatter.29.cloned.1.call-update) | async-done | bytes 6160 | tf_op jit(solution)/shard_map/reduce_scatter | solution.py:242
  640.7 16.2 %add_convert_fusion = bf16[1536,2048]{1,0:T(8,128)(2,1)} fusion(f32[1536]{0:T(1024)S(1)} %negate_multiply_fusion.1, f32[1536]{0:T(1024)S(1)} %negate_multiply_fusion.2, f32[1536]{0:T(1024)S(1)} %get-tuple-element.412, f32[1536]{0:T(1024)S(1)} %copy-done.23, bf16[1536,2048]{1,0:T(8,128)(2,1)} %param.21, f32[1536]{0:T(1024)S(1)} %copy-done.31, ...), kind=kLoop, calls=%fused_computation.64 | loop fusion | flops 50331648 | bytes 37801984 | tf_op jit(solution)/shard_map/convert_element_type | solution.py:249
  658.3 7.9 fusion.108
  666.2 21.3 %add_convert_fusion.2 = bf16[1536,2048]{1,0:T(8,128)(2,1)} fusion(f32[1536,2048]{1,0:T(8,128)} %fusion.108, bf16[1536,2048]{1,0:T(8,128)(2,1)} %copy-done.52, bf16[2048,2048]{1,0:T(8,128)(2,1)} %all-gather.13.cloned.1.call-done), kind=kOutput, calls=%fused_computation.69 | convolution fusion | flops 12891193344 | bytes 33554432 | tf_op jit(solution)/shard_map/dot_general | solution.py:186
  688.1 24.7 %fusion.88 = f32[2048,2048]{1,0:T(8,128)} fusion(bf16[1536,2048]{1,0:T(8,128)(2,1)} %get-tuple-element.432, bf16[1536,2048]{1,0:T(8,128)(2,1)} %param.21, f32[2048]{0:T(1024)S(1)} %bitcast.339, f32[2048]{0:T(1024)S(1)} %bitcast.320, f32[1536]{0:T(1024)S(1)} %copy-done.31, f32[1536]{0:T(1024)S(1)} %copy-done.23), kind=kOutput, calls=%fused_computation.215 | convolution fusion | flops 12903776256 | bytes 29388800 | tf_op jit(solution)/shard_map/dot_general | solution.py:63
  712.9 9.2 convert_element_type.119
  725.9 47.2 %reduce-scatter.21.cloned.1.call-done = f32[256,1536]{1,0:T(8,128)} async-done(((f32[2048,1536]{1,0:T(8,128)}), f32[256,1536]{1,0:T(8,128)}) %reduce-scatter.21.cloned.1.call-update) | async-done | bytes 1572880 | tf_op jit(solution)/shard_map/reduce_scatter | solution.py:239
  773.1 4.7 add_multiply_fusion.2
  783.5 27.3 %reduce-scatter.33.cloned.1.call-done = f32[128,2]{1,0:T(8,128)} async-done(((f32[1024,2]{1,0:T(8,128)}), f32[128,2]{1,0:T(8,128)}) %reduce-scatter.33.cloned.1.call-update) | async-done | bytes 1040
  813.7 19.2 %reduce-scatter.35.cloned.1.call-done = bf16[64,4]{1,0:T(8,128)(2,1)} async-done(((bf16[256,4]{1,0:T(8,128)(2,1)}), bf16[64,4]{1,0:T(8,128)(2,1)}) %reduce-scatter.35.cloned.1.call-update) | async-done | bytes 528
  835.0 109.1 %reduce-scatter.19.cloned.1.call-done = bf16[1536,512]{1,0:T(8,128)(2,1)} async-done(((bf16[1536,2048]{1,0:T(8,128)(2,1)}), bf16[1536,512]{1,0:T(8,128)(2,1)}) %reduce-scatter.19.cloned.1.call-update) | async-done | bytes 1572880 | tf_op jit(solution)/shard_map/reduce_scatter | solution.py:248
  944.1 4.0 add_convert_fusion.5
  948.1 109.6 %reduce-scatter.17.cloned.1.call-done = bf16[1536,512]{1,0:T(8,128)(2,1)} async-done(((bf16[1536,2048]{1,0:T(8,128)(2,1)}), bf16[1536,512]{1,0:T(8,128)(2,1)}) %reduce-scatter.17.cloned.1.call-update) | async-done | bytes 1572880 | tf_op jit(solution)/shard_map/reduce_scatter | solution.py:189
  1057.7 4.0 multiply_convert_fusion.2
  1061.7 116.8 %reduce-scatter.25.cloned.1.call-done = f32[256,2048]{1,0:T(8,128)} async-done(((f32[2048,2048]{1,0:T(8,128)}), f32[256,2048]{1,0:T(8,128)}) %reduce-scatter.25.cloned.1.call-update) | async-done | bytes 2097168 | tf_op jit(solution)/shard_map/reduce_scatter | solution.py:243
  1178.4 5.7 add_multiply_fusion.1
  (276 shorter events, 107.2 us)
Async XLA Ops:
  7.2 15.7 %copy-start.35 = (f32[6,64]{1,0:T(8,128)S(1)}, f32[6,64]{1,0:T(8,128)}, u32[]{:S(2)}) copy-start(f32[6,64]{1,0:T(8,128)} %param.36) | copy-start | bytes 4612
  7.2 84.9 %copy-start.50 = (s32[3]{0:T(128)S(1)}, s32[3]{0:T(128)}, u32[]{:S(2)}) copy-start(s32[3]{0:T(128)} %param.23) | copy-start | bytes 40
  7.2 85.0 %copy-start.48 = (f32[2,128]{1,0:T(2,128)S(1)}, f32[2,128]{1,0:T(2,128)}, u32[]{:S(2)}) copy-start(f32[2,128]{1,0:T(2,128)} %param.32) | copy-start | bytes 3076
  7.2 104.9 %all-gather.7.cloned.1.call-start = ((), (), s32[]{:S(2)}) async-start(), calls=%async_computation.10 | async-start | bytes 7077888 | tf_op jit(solution)/shard_map/all_gather | solution.py:153
  9.7 221.0 %all-gather.11.cloned.1.call-start = ((), (), s32[]{:S(2)}) async-start(), calls=%async_computation.12 | async-start | bytes 9437184 | tf_op jit(solution)/shard_map/all_gather | solution.py:156
  12.5 288.9 %reduce-scatter.23.cloned.1.call-start = ((), (), s32[]{:S(2)}) async-start(), calls=%async_computation.17 | async-start | bytes 4718592 | tf_op jit(solution)/shard_map/reduce_scatter | solution.py:241
  92.2 430.0 %copy-start.28 = (f32[1536]{0:T(1024)}, f32[1536]{0:T(1024)S(1)}, u32[]{:S(2)}) copy-start(f32[1536]{0:T(1024)S(1)} %reshape.412) | copy-start | bytes 18436
  105.0 125.7 %copy-start.22 = (f32[1536]{0:T(1024)}, f32[1536]{0:T(1024)S(1)}, u32[]{:S(2)}) copy-start(f32[1536]{0:T(1024)S(1)} %broadcast_multiply_fusion) | copy-start | bytes 18436
  109.6 121.1 %copy-start.30 = (f32[1536]{0:T(1024)}, f32[1536]{0:T(1024)S(1)}, u32[]{:S(2)}) copy-start(f32[1536]{0:T(1024)S(1)} %fusion.64) | copy-start | bytes 18436
  111.4 67.5 %copy-start.9 = (f32[512,32]{1,0:T(8,128)}, f32[512,32]{1,0:T(8,128)S(1)}, u32[]{:S(2)}) copy-start(f32[512,32]{1,0:T(8,128)S(1)} %get-tuple-element.428) | copy-start | bytes 196612
  112.1 16.1 %copy-start.26 = (f32[1,2048]{1,0:T(1,128)}, f32[1,2048]{1,0:T(1,128)S(1)}, u32[]{:S(2)}) copy-start(f32[1,2048]{1,0:T(1,128)S(1)} %get-tuple-element.411) | copy-start | bytes 24580
  112.1 16.1 %copy-start.39 = (f32[1,2048]{1,0:T(1,128)}, f32[1,2048]{1,0:T(1,128)S(1)}, u32[]{:S(2)}) copy-start(f32[1,2048]{1,0:T(1,128)S(1)} %get-tuple-element.410) | copy-start | bytes 24580
  112.1 118.6 %copy-start.24 = (f32[1,2048]{1,0:T(1,128)}, f32[1,2048]{1,0:T(1,128)S(1)}, u32[]{:S(2)}) copy-start(f32[1,2048]{1,0:T(1,128)S(1)} %get-tuple-element.409) | copy-start | bytes 24580
  112.1 118.6 %copy-start.37 = (f32[1,2048]{1,0:T(1,128)}, f32[1,2048]{1,0:T(1,128)S(1)}, u32[]{:S(2)}) copy-start(f32[1,2048]{1,0:T(1,128)S(1)} %get-tuple-element.408) | copy-start | bytes 24580
  151.8 20.4 %copy-start.3 = (bf16[3,512,2,1,256]{4,3,2,1,0:T(2,128)(2,1)}, bf16[3,512,2,1,256]{4,3,2,1,0:T(2,128)(2,1)S(1)}, u32[]{:S(2)}) copy-start(bf16[3,512,2,1,256]{4,3,2,1,0:T(2,128)(2,1)S(1)} %slice.258) | copy-start | bytes 4718596
  230.6 184.0 %reduce-scatter.27.cloned.1.call-start = ((), (), s32[]{:S(2)}) async-start(), calls=%async_computation.19 | async-start | bytes 18874368 | tf_op jit(solution)/shard_map/reduce_scatter | solution.py:245
  301.2 113.4 %copy-start.11 = (f32[2048,256]{1,0:T(8,128)S(1)}, f32[2048,256]{1,0:T(8,128)}, u32[]{:S(2)}) copy-start(f32[2048,256]{1,0:T(8,128)} %param.34) | copy-start | bytes 6291460
  301.3 143.2 %all-gather.9.cloned.1.call-start = ((), (), s32[]{:S(2)}) async-start(), calls=%async_computation.11 | async-start | bytes 2359296 | tf_op jit(solution)/shard_map/all_gather | solution.py:155
  305.3 116.3 %copy-start.10 = (f32[512,32]{1,0:T(8,128)S(1)}, f32[512,32]{1,0:T(8,128)}, u32[]{:S(2)}) copy-start(f32[512,32]{1,0:T(8,128)} %copy-done.9) | copy-start | bytes 196612
  305.3 116.4 %copy-start.20 = (f32[512,32]{1,0:T(8,128)S(1)}, f32[512,32]{1,0:T(8,128)}, u32[]{:S(2)}) copy-start(f32[512,32]{1,0:T(8,128)} %get-tuple-element.426) | copy-start | bytes 196612
  305.3 216.8 %all-gather.13.cloned.1.call-start = ((), (), s32[]{:S(2)}) async-start(), calls=%async_computation.13 | async-start | bytes 9437184 | tf_op jit(solution)/shard_map/all_gather | solution.py:158
  421.6 217.6 %reduce-scatter.29.cloned.1.call-start = ((), (), s32[]{:S(2)}) async-start(), calls=%async_computation.20 | async-start | bytes 73728 | tf_op jit(solution)/shard_map/reduce_scatter | solution.py:242
  432.9 23.4 %copy-start.1 = (bf16[3,512,2,256]{3,1,2,0:T(8,128)(2,1)S(1)}, bf16[3,512,2,256]{3,1,2,0:T(8,128)(2,1)}, u32[]{:S(2)}) copy-start(bf16[3,512,2,256]{3,1,2,0:T(8,128)(2,1)} %copy-done) | copy-start | bytes 4718596
  432.9 23.4 %copy-start.2 = (bf16[3,512,2,256]{3,1,2,0:T(8,128)(2,1)S(1)}, bf16[3,512,2,256]{3,1,2,0:T(8,128)(2,1)}, u32[]{:S(2)}) copy-start(bf16[3,512,2,256]{3,1,2,0:T(8,128)(2,1)} %get-tuple-element.625) | copy-start | bytes 4718596
  432.9 23.4 %copy-start.51 = (s32[3]{0:T(128)S(1)}, s32[3]{0:T(128)}, u32[]{:S(2)}) copy-start(s32[3]{0:T(128)} %param.23) | copy-start | bytes 40
  549.1 19.3 %copy-start.23 = (f32[1536]{0:T(1024)S(1)}, f32[1536]{0:T(1024)}, u32[]{:S(2)}) copy-start(f32[1536]{0:T(1024)} %copy-done.22) | copy-start | bytes 18436
  549.1 19.3 %copy-start.25 = (f32[1,2048]{1,0:T(1,128)S(1)}, f32[1,2048]{1,0:T(1,128)}, u32[]{:S(2)}) copy-start(f32[1,2048]{1,0:T(1,128)} %copy-done.24) | copy-start | bytes 24580
  549.1 19.3 %copy-start.27 = (f32[1,2048]{1,0:T(1,128)S(1)}, f32[1,2048]{1,0:T(1,128)}, u32[]{:S(2)}) copy-start(f32[1,2048]{1,0:T(1,128)} %copy-done.26) | copy-start | bytes 24580
  568.4 22.2 %copy-start.34 = (f32[1536]{0:T(1024)S(1)}, f32[1536]{0:T(1024)}, u32[]{:S(2)}) copy-start(f32[1536]{0:T(1024)} %copy-done.33) | copy-start | bytes 18436
  568.4 22.2 %copy-start.31 = (f32[1536]{0:T(1024)S(1)}, f32[1536]{0:T(1024)}, u32[]{:S(2)}) copy-start(f32[1536]{0:T(1024)} %copy-done.30) | copy-start | bytes 18436
  590.6 14.2 %copy-start.32 = (f32[2048]{0:T(1024)S(1)}, f32[2048]{0:T(1024)}, u32[]{:S(2)}) copy-start(f32[2048]{0:T(1024)} %get-tuple-element.376) | copy-start | bytes 24580
  590.6 16.4 %copy-start.40 = (f32[1,2048]{1,0:T(1,128)S(1)}, f32[1,2048]{1,0:T(1,128)}, u32[]{:S(2)}) copy-start(f32[1,2048]{1,0:T(1,128)} %copy-done.39) | copy-start | bytes 24580
  605.5 118.4 %reduce-scatter.31.cloned.1.call-start = ((), (), s32[]{:S(2)}) async-start(), calls=%async_computation.21 | async-start | bytes 442368
  606.9 166.2 %reduce-scatter.21.cloned.1.call-start = ((), (), s32[]{:S(2)}) async-start(), calls=%async_computation.16 | async-start | bytes 14155776 | tf_op jit(solution)/shard_map/reduce_scatter | solution.py:239
  623.7 187.1 %reduce-scatter.33.cloned.1.call-start = ((), (), s32[]{:S(2)}) async-start(), calls=%async_computation.22 | async-start | bytes 589824
  624.8 208.2 %reduce-scatter.35.cloned.1.call-start = ((), (), s32[]{:S(2)}) async-start(), calls=%async_computation.23 | async-start | bytes 81920
  640.7 303.4 %reduce-scatter.19.cloned.1.call-start = ((), (), s32[]{:S(2)}) async-start(), calls=%async_computation.15 | async-start | bytes 7864320 | tf_op jit(solution)/shard_map/reduce_scatter | solution.py:248
  656.9 400.8 %reduce-scatter.17.cloned.1.call-start = ((), (), s32[]{:S(2)}) async-start(), calls=%async_computation.14 | async-start | bytes 7864320 | tf_op jit(solution)/shard_map/reduce_scatter | solution.py:189
  687.4 491.0 %reduce-scatter.25.cloned.1.call-start = ((), (), s32[]{:S(2)}) async-start(), calls=%async_computation.18 | async-start | bytes 18874368 | tf_op jit(solution)/shard_map/reduce_scatter | solution.py:243
  712.9 11.9 copy-start.44
  712.9 60.3 %copy-start.8 = (f32[256,1536]{1,0:T(8,128)S(1)}, f32[256,1536]{1,0:T(8,128)}, u32[]{:S(2)}) copy-start(f32[256,1536]{1,0:T(8,128)} %param.24) | copy-start | bytes 4718596
  724.7 53.1 %copy-start.43 = (f32[2,96]{1,0:T(2,128)}, f32[2,96]{1,0:T(2,128)S(1)}, u32[]{:S(2)}) copy-start(f32[2,96]{1,0:T(2,128)S(1)} %copy.188) | copy-start | bytes 2308
  779.7 32.0 %copy-start.45 = (f32[2,2,128]{2,1,0:T(2,128)S(1)}, f32[2,2,128]{2,1,0:T(2,128)}, u32[]{:S(2)}) copy-start(f32[2,2,128]{2,1,0:T(2,128)} %param.33) | copy-start | bytes 6148
  779.7 32.0 %copy-start.49 = (f32[2,128]{1,0:T(2,128)S(1)}, f32[2,128]{1,0:T(2,128)}, u32[]{:S(2)}) copy-start(f32[2,128]{1,0:T(2,128)} %param.32) | copy-start | bytes 3076
  779.7 54.7 %copy-start.36 = (f32[6,64]{1,0:T(8,128)S(1)}, f32[6,64]{1,0:T(8,128)}, u32[]{:S(2)}) copy-start(f32[6,64]{1,0:T(8,128)} %param.36) | copy-start | bytes 4612
  783.5 274.2 %copy-start.29 = (f32[1536]{0:T(1024)S(1)}, f32[1536]{0:T(1024)}, u32[]{:S(2)}) copy-start(f32[1536]{0:T(1024)} %copy-done.28) | copy-start | bytes 18436
  811.7 250.0 %copy-start.42 = (f32[2,128]{1,0:T(2,128)}, f32[2,128]{1,0:T(2,128)S(1)}, u32[]{:S(2)}) copy-start(f32[2,128]{1,0:T(2,128)S(1)} %copy.190) | copy-start | bytes 3076
  948.1 230.3 %copy-start.5 = (f32[256,2048]{1,0:T(8,128)S(1)}, f32[256,2048]{1,0:T(8,128)}, u32[]{:S(2)}) copy-start(f32[256,2048]{1,0:T(8,128)} %param.30) | copy-start | bytes 6291460
  (23 other events, 102.5 us)
Sparse Core Ops, SparseCore 0:
  10.5 48.2 all-gather.6
  61.2 54.3 all-gather.10
  230.7 48.3 reduce-scatter.22
  301.4 113.2 reduce-scatter.26
  416.3 28.1 all-gather.8
  446.8 55.8 all-gather.12
  605.6 33.5 reduce-scatter.28
  642.8 33.8 reduce-scatter.30
  680.8 92.2 reduce-scatter.20
  776.6 34.1 reduce-scatter.32
  813.6 19.2 reduce-scatter.34
  835.1 108.9 reduce-scatter.18
  946.4 111.2 reduce-scatter.16
  1061.7 116.7 reduce-scatter.24
where the time goes:
time: 1200 us; the launch traced here: 1190 us
  waiting for transfers between devices  565 us (47%)
  matrix products  267 us (22%)
  other arithmetic  130 us (11%)
  local copies, waits for them, and re-layouts  123 us (10%)
  blocking collectives  88.4 us (7%)
  between operations  14.9 us (1%)
    reduce_scatter x1, waiting for transfers between devices, on_device(): lax.psum_scatter(expand_local, 'dp', scatter_dimension=0, tiled=True)  117 us
    reduce_scatter x1, waiting for transfers between devices, on_device(): lax.psum_scatter(partial_sum.astype(jnp.bfloat16), 'tensor', scatter_dime...  110 us
    reduce_scatter x1, waiting for transfers between devices, on_device(): lax.psum_scatter(shrink_local, 'dp', scatter_dimension=1, tiled=True)  109 us
    reduce_scatter x1, waiting for transfers between devices, on_device(): lax.psum_scatter((dinput_one + dinput_two).astype(jnp.bfloat16), 'tensor'...  109 us
    dot_general x4, matrix products, contract_cols(): lax.dot_general(left, right, (((1,), (1,)), ((), ())), preferred_element_...  76.4 us
    all_gather x1, blocking collectives, on_device(): lax.all_gather(vectors.astype(jnp.bfloat16), ('dp', 'tensor'), axis=1, ti...  69.1 us
    dot_general x4, matrix products, contract_rows(): lax.dot_general(left, right, (((0,), (0,)), ((), ())), preferred_element_...  68.9 us
    dot_general x1, matrix products, on_device(): jnp.dot(normed_two, expand, preferred_element_type=jnp.float32)  48.2 us
  transfers between devices with their start and end apart: 14, of which 9 were waited for; matrix products, arithmetic and copies ran while one was open for 35% of the time, Pallas kernels for 0%

commit v1 on v0

v1 whole, which is shorter than its diff:
```python
import functools
import math

import jax
import jax.numpy as jnp
from jax import lax
from jax.experimental import pallas as pl
from jax.experimental.pallas import tpu as pltpu
from jax.sharding import PartitionSpec as P

HD = 256
ROT = 64
SEQ_LEN = 512
STEP = 10

layer_eps = 1e-05
adam_eps = 1e-08
beta_one = 0.9
beta_two = 0.95
learn_rate = 0.02
decay_rate = 0.01
rotary_base = 10000.0

TILE = 128
BLOCK = 256
SLOT_TILES = SEQ_LEN // TILE
LEAST = 3
VMEM = 60 * 1024 * 1024
F32 = jnp.float32
BF16 = jnp.bfloat16

GATHER = "sc"
REDUCE = "sc"


def rotary_tables():
    half = ROT // 2
    frequency = jnp.exp(jnp.arange(half, dtype=F32) * (-2.0 * math.log(rotary_base) / ROT))
    angles = jnp.arange(SEQ_LEN, dtype=F32)[:, None] * frequency[None, :]
    cos, sin = jnp.cos(angles), jnp.sin(angles)
    zero = jnp.zeros((SEQ_LEN, half), F32)
    rest = jnp.ones((SEQ_LEN, 128 - ROT), F32)
    pad = jnp.zeros((SEQ_LEN, 128 - ROT), F32)
    return jnp.stack(
        [
            jnp.concatenate([cos, cos, rest], 1),
            jnp.concatenate([-sin, zero, pad], 1),
            jnp.concatenate([zero, sin, pad], 1),
        ]
    )


def turn(values, table_ref, rows, sign):
    head = values[:, :128]
    ahead = pltpu.roll(head, 128 - ROT // 2, 1)
    behind = pltpu.roll(head, ROT // 2, 1)
    swing = ahead * table_ref[1, rows, :] + behind * table_ref[2, rows, :]
    turned = head * table_ref[0, rows, :]
    turned = turned + swing if sign > 0 else turned - swing
    return jnp.concatenate([turned, values[:, 128:]], axis=1)


def slot_tiles(lens_ref, slot):
    return (lens_ref[slot] + (TILE - 1)) // TILE


def live_tiles(lens_ref, slots):
    total = slot_tiles(lens_ref, 0)
    for slot in range(1, slots):
        total = total + slot_tiles(lens_ref, slot)
    return total


def live_blocks(lens_ref, slots):
    return jnp.maximum((live_tiles(lens_ref, slots) + 1) // 2, LEAST)


def source_tile(lens_ref, index, slots):
    start = 0
    source = 0
    for slot in range(slots):
        count = slot_tiles(lens_ref, slot)
        inside = (index >= start) & (index < start + count)
        source = jnp.where(inside, slot * SLOT_TILES + index - start, source)
        start = start + count
    return source


def compact_tile(lens_ref, source, slots):
    slot = source // SLOT_TILES
    within = source % SLOT_TILES
    start = 0
    target = -1
    for other in range(slots):
        count = slot_tiles(lens_ref, other)
        target = jnp.where((slot == other) & (within < count), start + within, target)
        start = start + count
    return target


def norm_parts(values):
    average = jnp.mean(values, axis=-1, keepdims=True)
    centred = values - average
    variance = jnp.mean(centred * centred, axis=-1, keepdims=True)
    return centred, lax.rsqrt(variance + layer_eps)


def norm_rows(lens, layer_input, cotangent, vecs, slots):
    rows, width = layer_input.shape
    tiles = rows // TILE

    def kernel(lens_ref, x_ref, cot_ref, vec_ref, one_ref, two_ref, x_out, up_out):
        i = pl.program_id(0)
        total = live_tiles(lens_ref, slots)
        last = 2 * live_blocks(lens_ref, slots)

        @pl.when(i < total)
        def _():
            source = source_tile(lens_ref, i, slots)
            values = x_ref[...].astype(F32)
            centred, scale = norm_parts(values)
            hat = centred * scale
            one_ref[...] = (hat * vec_ref[0:1, :] + vec_ref[1:2, :]).astype(BF16)
            two_ref[...] = (hat * vec_ref[2:3, :] + vec_ref[3:4, :]).astype(BF16)
            x_out[...] = x_ref[...]
            length = lens_ref[source // SLOT_TILES]
            place = (source % SLOT_TILES) * TILE + lax.broadcasted_iota(jnp.int32, (TILE, 1), 0)
            up_out[...] = jnp.where(place < length, cot_ref[...].astype(F32), 0.0).astype(BF16)

        @pl.when((i >= total) & (i < last))
        def _():
            for ref in (one_ref, two_ref, x_out, up_out):
                ref[...] = jnp.zeros_like(ref)

    def reads(i, lens_ref):
        total = jnp.maximum(live_tiles(lens_ref, slots), 1)
        return (source_tile(lens_ref, jnp.minimum(i, total - 1), slots), 0)

    def writes(i, lens_ref):
        return (jnp.minimum(i, 2 * live_blocks(lens_ref, slots) - 1), 0)

    shape = jax.ShapeDtypeStruct((rows, width), BF16)
    return pl.pallas_call(
        kernel,
        out_shape=(shape,) * 4,
        grid_spec=pltpu.PrefetchScalarGridSpec(
            num_scalar_prefetch=1,
            grid=(tiles,),
            in_specs=[
                pl.BlockSpec((TILE, width), reads),
                pl.BlockSpec((TILE, width), reads),
                pl.BlockSpec(vecs.shape, lambda i, lens_ref: (0, 0)),
            ],
            out_specs=[pl.BlockSpec((TILE, width), writes)] * 4,
        ),
        compiler_params=pltpu.CompilerParams(vmem_limit_bytes=VMEM),
        cost_estimate=pl.CostEstimate(
            flops=rows * width * 8, bytes_accessed=rows * width * 12, transcendentals=0
        ),
        name="norm_rows",
    )(lens, layer_input, cotangent, vecs)


class Gathered:
    def __init__(self, pieces, shard):
        self.pieces = [piece for piece, _, _ in pieces]
        self.places = [(mask, extra) for _, mask, extra in pieces]
        self.shard = shard
        self.width = self.pieces[0].shape[1]

    def copies(self, refs, target, sems):
        if self.places[0][0] is not None:
            me = lax.axis_index("dp")
        out = []
        for index, (ref, (mask, extra)) in enumerate(zip(refs, self.places)):
            count = ref.shape[0]
            start = 0 if mask is None else (me ^ mask) * self.shard + extra
            start = start if mask is None else pl.multiple_of(start, count)
            out.append(
                pltpu.make_async_copy(ref, target.at[pl.ds(start, count), :], sems.at[index])
            )
        return out


def any_specs(count):
    return [pl.BlockSpec(memory_space=pl.ANY)] * count


def project_rows(lens, normed, upstream, weights, shift_row, table, slots, qkv_width):
    rows, width = normed.shape
    att_width = weights.width - qkv_width
    blocks = rows // BLOCK
    count = len(weights.pieces)

    def kernel(lens_ref, n_ref, up_ref, shift_ref, table_ref, *rest):
        refs, (qkv_ref, back_ref, held, sems) = rest[:count], rest[count:]
        i = pl.program_id(0)

        @pl.when(i == 0)
        def _():
            copies = weights.copies(refs, held, sems)
            for copy in copies:
                copy.start()
            for copy in copies:
                copy.wait()

        @pl.when(i < live_blocks(lens_ref, slots))
        def _():
            for piece in range(qkv_width // HD):
                cols = slice(piece * HD, (piece + 1) * HD)
                part = jnp.dot(n_ref[...], held[:, cols], preferred_element_type=F32)
                part = part + shift_ref[0:1, cols]
                if piece % 3 == 2:
                    qkv_ref[:, cols] = part.astype(BF16)
                    continue
                for half in range(BLOCK // TILE):
                    tile = slice(half * TILE, (half + 1) * TILE)
                    source = source_tile(lens_ref, i * (BLOCK // TILE) + half, slots)
                    place = pl.multiple_of((source % SLOT_TILES) * TILE, TILE)
                    qkv_ref[tile, cols] = turn(
                        part[tile], table_ref, pl.ds(place, TILE), 1
                    ).astype(BF16)
            back_ref[...] = jnp.dot(
                up_ref[...], held[:, qkv_width:], preferred_element_type=F32
            ).astype(BF16)

    def block(i, lens_ref):
        return (jnp.minimum(i, live_blocks(lens_ref, slots) - 1), 0)

    whole2 = lambda i, lens_ref: (0, 0)
    return pl.pallas_call(
        kernel,
        out_shape=(
            jax.ShapeDtypeStruct((rows, qkv_width), BF16),
            jax.ShapeDtypeStruct((rows, att_width), BF16),
        ),
        grid_spec=pltpu.PrefetchScalarGridSpec(
            num_scalar_prefetch=1,
            grid=(blocks,),
            in_specs=[
                pl.BlockSpec((BLOCK, width), block),
                pl.BlockSpec((BLOCK, width), block),
                pl.BlockSpec(shift_row.shape, whole2),
                pl.BlockSpec(table.shape, lambda i, lens_ref: (0, 0, 0)),
            ]
            + any_specs(count),
            out_specs=[
                pl.BlockSpec((BLOCK, qkv_width), block),
                pl.BlockSpec((BLOCK, att_width), block),
            ],
            scratch_shapes=[
                pltpu.VMEM((width, weights.width), BF16),
                pltpu.SemaphoreType.DMA((count,)),
            ],
        ),
        compiler_params=pltpu.CompilerParams(vmem_limit_bytes=VMEM),
        cost_estimate=pl.CostEstimate(
            flops=2 * rows * width * weights.width,
            bytes_accessed=rows * width * 8,
            transcendentals=0,
        ),
        name="project_rows",
    )(lens, normed, upstream, shift_row, table, *weights.pieces)


def attend(lens, qkv, back, table, slots):
    rows, qkv_width = qkv.shape
    heads = qkv_width // (3 * HD)
    scale = HD ** (-0.5)

    def kernel(lens_ref, qkv_ref, back_ref, table_ref, att_ref, grad_ref, sum_ref, dk_acc, dv_acc):
        slot = pl.program_id(1)
        start = 0
        count = 0
        length = 0
        total = 0
        for other in range(slots):
            own = slot_tiles(lens_ref, other)
            start = jnp.where(other < slot, start + own, start)
            count = jnp.where(other == slot, own, count)
            length = jnp.where(other == slot, lens_ref[other], length)
            total = total + own
        limit = jnp.maximum(length, 1)

        @pl.when(slot == 0)
        def _():
            sum_ref[...] = jnp.zeros_like(sum_ref)
            for index in range(2 * LEAST + 6):
                if index * TILE < rows:
                    dead = (index >= total) & (index < 2 * live_blocks(lens_ref, slots))

                    @pl.when(dead)
                    def _(index=index):
                        tile = slice(index * TILE, (index + 1) * TILE)
                        att_ref[tile, :] = jnp.zeros((TILE, HD), BF16)
                        grad_ref[tile, :] = jnp.zeros((TILE, 3 * HD), BF16)

        base = start * TILE
        dot_nt = lambda a, b: lax.dot_general(
            a, b, (((1,), (1,)), ((), ())), preferred_element_type=F32
        )
        dot_tn = lambda a, b: lax.dot_general(
            a, b, (((0,), (0,)), ((), ())), preferred_element_type=F32
        )

        def keep_sum(value, cols):
            sum_ref[0:1, cols] += jnp.sum(value.astype(F32), axis=0, keepdims=True)

        for i in range(SLOT_TILES):

            @pl.when(count > i)
            def _(i=i):
                span = (i + 1) * TILE
                mine = pl.ds(pl.multiple_of(base + i * TILE, TILE), TILE)
                seen = pl.ds(pl.multiple_of(base, TILE), span)
                query = qkv_ref[mine, 0:HD]
                keys = qkv_ref[seen, HD : 2 * HD]
                values = qkv_ref[seen, 2 * HD : 3 * HD]
                push = back_ref[mine, :]
                place = i * TILE + lax.broadcasted_iota(jnp.int32, (TILE, span), 0)
                column = lax.broadcasted_iota(jnp.int32, (TILE, span), 1)
                allowed = (column <= place) & (column < limit)
                scores = jnp.where(allowed, dot_nt(query, keys) * scale, -1e30)
                powers = jnp.exp(scores - jnp.max(scores, axis=-1, keepdims=True))
                weights = powers / jnp.sum(powers, axis=-1, keepdims=True)
                low = weights.astype(BF16)
                att_ref[mine, :] = jnp.dot(low, values, preferred_element_type=F32).astype(BF16)
                pushed = dot_nt(push, values)
                inner = jnp.sum(weights * pushed, axis=-1, keepdims=True)
                dscores = (weights * (pushed - inner)).astype(BF16)
                dquery = jnp.dot(dscores, keys, preferred_element_type=F32) * scale
                dquery = turn(dquery, table_ref, slice(i * TILE, span), -1).astype(BF16)
                grad_ref[mine, 0:HD] = dquery
                keep_sum(dquery, slice(0, HD))
                dkeys = dot_tn(dscores, query)
                dvalues = dot_tn(low, push)
                if i > 0:
                    dk_acc[0 : i * TILE, :] += dkeys[0 : i * TILE]
                    dv_acc[0 : i * TILE, :] += dvalues[0 : i * TILE]
                dk_acc[i * TILE : span, :] = dkeys[i * TILE : span]
                dv_acc[i * TILE : span, :] = dvalues[i * TILE : span]

        for i in range(SLOT_TILES):

            @pl.when(count > i)
            def _(i=i):
                tile = slice(i * TILE, (i + 1) * TILE)
                mine = pl.ds(pl.multiple_of(base + i * TILE, TILE), TILE)
                dkeys = turn(dk_acc[tile, :] * scale, table_ref, tile, -1).astype(BF16)
                dvalues = dv_acc[tile, :].astype(BF16)
                grad_ref[mine, HD : 2 * HD] = dkeys
                grad_ref[mine, 2 * HD : 3 * HD] = dvalues
                keep_sum(dkeys, slice(HD, 2 * HD))
                keep_sum(dvalues, slice(2 * HD, 3 * HD))

    by_head = lambda h, s, lens_ref: (0, h)
    return pl.pallas_call(
        kernel,
        out_shape=(
            jax.ShapeDtypeStruct((rows, heads * HD), BF16),
            jax.ShapeDtypeStruct((rows, qkv_width), BF16),
            jax.ShapeDtypeStruct((8, qkv_width), F32),
        ),
        grid_spec=pltpu.PrefetchScalarGridSpec(
            num_scalar_prefetch=1,
            grid=(heads, slots),
            in_specs=[
                pl.BlockSpec((rows, 3 * HD), by_head),
                pl.BlockSpec((rows, HD), by_head),
                pl.BlockSpec(table.shape, lambda h, s, lens_ref: (0, 0, 0)),
            ],
            out_specs=[
                pl.BlockSpec((rows, HD), by_head),
                pl.BlockSpec((rows, 3 * HD), by_head),
                pl.BlockSpec((8, 3 * HD), by_head),
            ],
            scratch_shapes=[pltpu.VMEM((SEQ_LEN, HD), F32), pltpu.VMEM((SEQ_LEN, HD), F32)],
        ),
        compiler_params=pltpu.CompilerParams(vmem_limit_bytes=VMEM),
        cost_estimate=pl.CostEstimate(
            flops=14 * heads * slots * SEQ_LEN * SEQ_LEN * HD,
            bytes_accessed=rows * qkv_width * 6,
            transcendentals=heads * slots * SEQ_LEN * SEQ_LEN,
        ),
        name="attend",
    )(lens, qkv, back, table)


def middle(lens, first, span, tensors, vecs, offset_row, entry, expand, shrink, carried, slots):
    normed, upstream, attended, dpacked, inputs = tensors
    rows, width = normed.shape
    hidden_width = expand.width
    qkv_width = dpacked.shape[1]
    att_width = attended.shape[1]
    counts = [len(entry.pieces), len(expand.pieces), len(shrink.pieces)]
    total = sum(counts)
    hold = 2 if carried is not None else 0
    chunk = 512
    nt = (((1,), (1,)), ((), ()))

    def kernel(lens_ref, n_ref, up_ref, att_ref, dp_ref, x_ref, vec_ref, off_ref, *rest):
        refs = rest[:total]
        rest = rest[total + hold :]
        act_ref, dh_ref, both_ref, sum_ref = rest[:4]
        held_e, held_x, held_s, done, dtwo, sems_e, sems_x, sems_s = rest[4:]
        i = pl.program_id(0)

        def fetch():
            a, b = counts[0], counts[0] + counts[1]
            return (
                expand.copies(refs[a:b], held_x, sems_x),
                shrink.copies(refs[b:], held_s, sems_s),
                entry.copies(refs[:a], held_e, sems_e),
            )

        @pl.when(i == 0)
        def _():
            sum_ref[...] = jnp.zeros_like(sum_ref)
            for group in fetch():
                for copy in group:
                    copy.start()
            for copy in fetch()[0]:
                copy.wait()
            for copy in fetch()[1]:
                copy.wait()
            for copy in fetch()[2]:
                copy.wait()

        @pl.when(first + i < live_blocks(lens_ref, slots))
        def _():
            for start in range(0, hidden_width, chunk):
                cols = slice(start, start + chunk)
                hidden = jnp.dot(n_ref[...], held_x[:, cols], preferred_element_type=F32)
                hidden = hidden + off_ref[0:1, cols]
                dact = jnp.dot(up_ref[...], held_s[:, cols], preferred_element_type=F32)
                below = 0.5 + 0.5 * lax.erf(hidden * (0.5**0.5))
                slope = below + hidden * (
                    jnp.exp(-0.5 * hidden * hidden) * ((2.0 * math.pi) ** -0.5)
                )
                act_ref[:, cols] = (hidden * below).astype(BF16)
                dhidden = (dact * slope).astype(BF16)
                dh_ref[:, cols] = dhidden
                sum_ref[5:6, cols] += jnp.sum(dhidden.astype(F32), axis=0, keepdims=True)
            values = x_ref[...].astype(F32)
            centred, scale = norm_parts(values)
            hat = centred * scale
            mean_e = jnp.zeros((BLOCK, 1), F32)
            mean_eh = jnp.zeros((BLOCK, 1), F32)
            for start in range(0, width, chunk):
                cols = slice(start, start + chunk)
                part = lax.dot_general(
                    att_ref[...], held_e[cols, qkv_width:], nt, preferred_element_type=F32
                ) + lax.dot_general(
                    act_ref[...], held_s[cols, :], nt, preferred_element_type=F32
                )
                both_ref[0, :, cols] = part.astype(BF16)
            for start in range(0, width, chunk):
                cols = slice(start, start + chunk)
                two = lax.dot_general(
                    dh_ref[...], held_x[cols, :], nt, preferred_element_type=F32
                )
                one = lax.dot_general(
                    dp_ref[...], held_e[cols, :qkv_width], nt, preferred_element_type=F32
                )
                part = hat[:, cols]
                sum_ref[0:1, cols] += jnp.sum(one * part, axis=0, keepdims=True)
                sum_ref[1:2, cols] += jnp.sum(one, axis=0, keepdims=True)
                sum_ref[2:3, cols] += jnp.sum(two * part, axis=0, keepdims=True)
                sum_ref[3:4, cols] += jnp.sum(two, axis=0, keepdims=True)
                sum_ref[4:5, cols] += jnp.sum(up_ref[:, cols].astype(F32), axis=0, keepdims=True)
                err = one * vec_ref[0:1, cols] + two * vec_ref[2:3, cols]
                done[:, cols] = err
                mean_e = mean_e + jnp.sum(err, axis=-1, keepdims=True)
                mean_eh = mean_eh + jnp.sum(err * part, axis=-1, keepdims=True)
            mean_e = mean_e * (1.0 / width)
            mean_eh = mean_eh * (1.0 / width)
            for start in range(0, width, chunk):
                cols = slice(start, start + chunk)
                both_ref[1, :, cols] = (
                    scale * (done[:, cols] - mean_e - hat[:, cols] * mean_eh)
                ).astype(BF16)

    def block(i, lens_ref):
        return (jnp.minimum(first + i, live_blocks(lens_ref, slots) - 1), 0)

    def local(i, lens_ref):
        top = jnp.maximum(live_blocks(lens_ref, slots) - 1 - first, 0)
        return (0, jnp.minimum(i, top), 0)

    def kept(i, lens_ref):
        top = jnp.maximum(live_blocks(lens_ref, slots) - 1, first)
        return (jnp.minimum(first + i, top), 0)

    whole2 = lambda i, lens_ref: (0, 0)
    sum_width = max(width, hidden_width)
    hidden_shape = jax.ShapeDtypeStruct((rows, hidden_width), BF16)
    args = [lens, normed, upstream, attended, dpacked, inputs, vecs, offset_row]
    args += entry.pieces + expand.pieces + shrink.pieces
    aliases = {}
    if carried is not None:
        aliases = {len(args): 0, len(args) + 1: 1}
        args += list(carried)
    return pl.pallas_call(
        kernel,
        out_shape=(
            hidden_shape,
            hidden_shape,
            jax.ShapeDtypeStruct((2, span * BLOCK, width), BF16),
            jax.ShapeDtypeStruct((8, sum_width), F32),
        ),
        grid_spec=pltpu.PrefetchScalarGridSpec(
            num_scalar_prefetch=1,
            grid=(span,),
            in_specs=[
                pl.BlockSpec((BLOCK, width), block),
                pl.BlockSpec((BLOCK, width), block),
                pl.BlockSpec((BLOCK, att_width), block),
                pl.BlockSpec((BLOCK, qkv_width), block),
                pl.BlockSpec((BLOCK, width), block),
                pl.BlockSpec(vecs.shape, whole2),
                pl.BlockSpec(offset_row.shape, whole2),
            ]
            + any_specs(total + hold),
            out_specs=[
                pl.BlockSpec((BLOCK, hidden_width), kept),
                pl.BlockSpec((BLOCK, hidden_width), kept),
                pl.BlockSpec((2, BLOCK, width), local),
                pl.BlockSpec((8, sum_width), whole2),
            ],
            scratch_shapes=[
                pltpu.VMEM((width, entry.width), BF16),
                pltpu.VMEM((width, expand.width), BF16),
                pltpu.VMEM((width, shrink.width), BF16),
                pltpu.VMEM((BLOCK, width), F32),
                pltpu.VMEM((8, 128), F32),
            ]
            + [pltpu.SemaphoreType.DMA((count,)) for count in (counts[1], counts[2], counts[0])][:0]
            + [
                pltpu.SemaphoreType.DMA((counts[0],)),
                pltpu.SemaphoreType.DMA((counts[1],)),
                pltpu.SemaphoreType.DMA((counts[2],)),
            ],
        ),
        input_output_aliases=aliases,
        compiler_params=pltpu.CompilerParams(vmem_limit_bytes=VMEM),
        cost_estimate=pl.CostEstimate(
            flops=2 * span * BLOCK * width * (4 * hidden_width + qkv_width + att_width),
            bytes_accessed=3 * width * hidden_width * 2 + span * BLOCK * width * 16,
            transcendentals=2 * span * BLOCK * hidden_width,
        ),
        name="middle",
    )(*args)


def gradient(lens, pairs, slots, shard, split):
    rows, width = pairs[0][0].shape
    blocks = width // shard
    sizes = [right.shape[1] for _, right in pairs]
    total = sum(sizes)
    half = blocks // 2
    most = rows // BLOCK

    def kernel(lens_ref, *rest):
        lefts = rest[: len(pairs)]
        rights = rest[len(pairs) : 2 * len(pairs)]
        outs = rest[2 * len(pairs) :]
        j = pl.program_id(0)
        live = live_blocks(lens_ref, slots)

        def emit(ref, depth):
            start = 0
            for left, right, size in zip(lefts, rights, sizes):
                ref[0, :, start : start + size] = lax.dot_general(
                    left[: depth * BLOCK, :],
                    right[: depth * BLOCK, :],
                    (((0,), (0,)), ((), ())),
                    preferred_element_type=F32,
                ).astype(BF16)
                start += size

        for depth in range(LEAST, most + 1):
            match = live == depth
            if split:
                for which, ref in enumerate(outs):
                    here = (j >= half) if which else (j < half)

                    @pl.when(match & here)
                    def _(ref=ref, depth=depth):
                        emit(ref, depth)

            else:

                @pl.when(match)
                def _(depth=depth):
                    emit(outs[0], depth)

    def left_block(j, lens_ref):
        if not split:
            return (0, j)
        mask = jnp.where(j < half, 2 * j + 1, 2 * (j - half))
        return (0, lens_ref[slots] ^ mask)

    whole2 = lambda j, lens_ref: (0, 0)
    if split:
        out_shape = [jax.ShapeDtypeStruct((half, shard, total), BF16)] * 2
        out_specs = [
            pl.BlockSpec((1, shard, total), lambda j, lens_ref: (jnp.minimum(j, half - 1), 0, 0)),
            pl.BlockSpec((1, shard, total), lambda j, lens_ref: (jnp.maximum(j - half, 0), 0, 0)),
        ]
    else:
        out_shape = [jax.ShapeDtypeStruct((blocks, shard, total), BF16)]
        out_specs = [pl.BlockSpec((1, shard, total), lambda j, lens_ref: (j, 0, 0))]
    return pl.pallas_call(
        kernel,
        out_shape=out_shape,
        grid_spec=pltpu.PrefetchScalarGridSpec(
            num_scalar_prefetch=1,
            grid=(blocks,),
            in_specs=[pl.BlockSpec((rows, shard), left_block) for _ in pairs]
            + [pl.BlockSpec(right.shape, whole2) for _, right in pairs],
            out_specs=out_specs,
        ),
        compiler_params=pltpu.CompilerParams(vmem_limit_bytes=VMEM),
        cost_estimate=pl.CostEstimate(
            flops=2 * rows * width * total,
            bytes_accessed=rows * (width + total) * 2 + width * total * 2,
            transcendentals=0,
        ),
        name="gradient",
    )(lens, *[left for left, _ in pairs], *[right for _, right in pairs])


def finish_rows(lens, layer_input, cotangent, summed, bias_row, slots):
    rows = layer_input.shape[0]
    width = summed.shape[2]
    tiles = rows // TILE

    def kernel(lens_ref, x_ref, cot_ref, sum_ref, bias_ref, out_ref, grad_ref):
        i = pl.program_id(0)
        target = compact_tile(lens_ref, i, slots)

        @pl.when(target >= 0)
        def _():
            length = lens_ref[i // SLOT_TILES]
            place = (i % SLOT_TILES) * TILE + lax.broadcasted_iota(jnp.int32, (TILE, 1), 0)
            live = place < length
            total = x_ref[...].astype(F32) + sum_ref[0].astype(F32) + bias_ref[0:1, :]
            out_ref[...] = jnp.where(live, total, 0.0).astype(BF16)
            grad = cot_ref[...].astype(F32) + sum_ref[1].astype(F32)
            grad_ref[...] = jnp.where(live, grad, 0.0).astype(BF16)

        @pl.when(target < 0)
        def _():
            out_ref[...] = jnp.zeros_like(out_ref)
            grad_ref[...] = jnp.zeros_like(grad_ref)

    def own(i, lens_ref):
        return (i, lens_ref[slots + 1])

    def packed(i, lens_ref):
        return (0, jnp.maximum(compact_tile(lens_ref, i, slots), 0), 0)

    shape = jax.ShapeDtypeStruct((rows, width), BF16)
    return pl.pallas_call(
        kernel,
        out_shape=(shape, shape),
        grid_spec=pltpu.PrefetchScalarGridSpec(
            num_scalar_prefetch=1,
            grid=(tiles,),
            in_specs=[
                pl.BlockSpec((TILE, width), own),
                pl.BlockSpec((TILE, width), own),
                pl.BlockSpec((2, TILE, width), packed),
                pl.BlockSpec(bias_row.shape, lambda i, lens_ref: (0, 0)),
            ],
            out_specs=[pl.BlockSpec((TILE, width), lambda i, lens_ref: (i, 0))] * 2,
        ),
        cost_estimate=pl.CostEstimate(
            flops=rows * width * 4, bytes_accessed=rows * width * 12, transcendentals=0
        ),
        name="finish_rows",
    )(lens, layer_input, cotangent, summed, bias_row)


def adamw(master, moments, gradient):
    first_moment = beta_one * moments[0] + (1.0 - beta_one) * gradient
    root_moment = jnp.sqrt(
        beta_two * moments[1] * moments[1] + (1.0 - beta_two) * gradient * gradient
    )
    first_hat = first_moment / (1.0 - beta_one**STEP)
    root_hat = root_moment / math.sqrt(1.0 - beta_two**STEP)
    update = -learn_rate * (first_hat / (root_hat + adam_eps) + decay_rate * master)
    return (jnp.stack([first_moment, root_moment]), update)


def swap(values, mask, size):
    return lax.ppermute(values, "dp", [(i, i ^ mask) for i in range(size)])


def after(values, *others):
    return lax.optimization_barrier((values, *others))[0]


def gather_weight(own):
    size = lax.axis_size("dp")
    return Gathered([(lax.all_gather(own, "dp", axis=0, tiled=True), None, 0)], own.shape[0])


def reduce_pieces(pieces):
    return lax.psum_scatter(pieces[0], "dp", scatter_dimension=0, tiled=True)[0].astype(F32)


def on_device(
    layer_input,
    cotangent,
    lengths,
    projector,
    projector_moments,
    shifts,
    shifts_moments,
    combiner,
    combiner_moments,
    expander,
    expander_moments,
    offsets,
    offsets_moments,
    reducer,
    reducer_moments,
    vectors,
    vectors_moments,
):
    dp, tensor = lax.axis_size("dp"), lax.axis_size("tensor")
    rank, lane = lax.axis_index("dp"), lax.axis_index("tensor")
    slots = lengths.shape[0]
    rows, width = layer_input.shape
    shard = projector.shape[0]
    qkv_width = projector.shape[1]
    att_width = combiner.shape[0]
    hidden_width = expander.shape[1]
    lens = jnp.concatenate(
        [lengths, jnp.stack([rank, lane]).astype(jnp.int32), jnp.zeros((3,), jnp.int32)]
    )
    table = rotary_tables()

    entry_own = jnp.concatenate([projector.astype(BF16), combiner.astype(BF16).T], axis=1)
    expand_own = expander.astype(BF16)
    shrink_own = reducer.astype(BF16).T

    sizes = [vectors.size, shifts.size, offsets.size]
    small = jnp.concatenate([vectors.reshape(-1), shifts.reshape(-1), offsets.reshape(-1)])
    small = jnp.pad(small, (0, -small.size % 1024)).astype(BF16).reshape(1, -1)
    small = lax.all_gather(small, ("dp", "tensor"), axis=0, tiled=True).astype(F32)
    full_vectors = (
        small[:, : sizes[0]].reshape(dp * tensor, *vectors.shape).transpose(1, 0, 2).reshape(6, -1)
    )
    biases = lax.dynamic_index_in_dim(
        small.reshape(dp, tensor, -1), lane, axis=1, keepdims=False
    )
    shift_row = (
        biases[:, sizes[0] : sizes[0] + sizes[1]]
        .reshape(dp, *shifts.shape)
        .transpose(1, 0, 2)
        .reshape(1, -1)
    )
    offset_row = (
        biases[:, sizes[0] + sizes[1] : sum(sizes)]
        .reshape(dp, *offsets.shape)
        .transpose(1, 0, 2)
        .reshape(1, -1)
    )
    vecs = jnp.pad(full_vectors, ((0, 2), (0, 0)))

    entry = gather_weight(entry_own)
    expand = gather_weight(expand_own)
    shrink = gather_weight(shrink_own)

    normed_one, normed_two, inputs, upstream = norm_rows(lens, layer_input, cotangent, vecs, slots)
    qkv, back = project_rows(
        lens, normed_one, upstream, entry, shift_row, table, slots, qkv_width
    )
    attended, dpacked, shift_sum = attend(lens, qkv, back, table, slots)
    split = False
    entry_parts = gradient(lens, [(normed_one, dpacked), (upstream, attended)], slots, shard, split)

    blocks = rows // BLOCK
    tensors = (normed_two, upstream, attended, dpacked, inputs)
    carried = None
    sums = 0.0
    reduced = []
    first = 0
    for span in (1, 2, blocks - 3):
        act, dhid, both, part = middle(
            lens, first, span, tensors, vecs, offset_row, entry, expand, shrink, carried, slots
        )
        carried = (act, dhid)
        sums = sums + part
        first += span
        reduced.append(
            lax.psum_scatter(both, "tensor", scatter_dimension=2, tiled=True)
        )
    shrink_parts = gradient(lens, [(upstream, act)], slots, shard, split)
    expand_parts = gradient(lens, [(normed_two, dhid)], slots, shard, split)

    entry_share = reduce_pieces(entry_parts)
    shrink_share = reduce_pieces(shrink_parts)
    expand_share = reduce_pieces(expand_parts)
    projector_grad = entry_share[:, :qkv_width]
    combiner_grad = entry_share[:, qkv_width:].T
    reducer_grad = shrink_share.T
    expander_grad = expand_share

    shift_part = shift_sum[0].reshape(shifts.shape[0], dp, -1).transpose(1, 0, 2).reshape(dp, -1)
    offset_part = (
        sums[5, :hidden_width].reshape(offsets.shape[0], dp, -1).transpose(1, 0, 2).reshape(dp, -1)
    )
    vector_part = sums[:5, :width].reshape(5, dp, -1).transpose(1, 0, 2).reshape(dp, -1)
    packed = jnp.concatenate([vector_part, shift_part, offset_part], axis=1)
    used = packed.shape[1]
    packed = jnp.pad(packed, ((0, 0), (0, -used % 1024)))
    packed = lax.psum_scatter(packed, "dp", scatter_dimension=0, tiled=True)[0]
    vector_part = packed[: vector_part.shape[1]].reshape(5, tensor, -1)
    begin = vector_part.size
    shifts_grad = packed[begin : begin + shifts.size].reshape(shifts.shape)
    offsets_grad = packed[begin + shifts.size : used].reshape(offsets.shape)
    norm_grad = lax.psum_scatter(
        vector_part[:4].transpose(1, 0, 2).reshape(tensor, -1),
        "tensor",
        scatter_dimension=0,
        tiled=True,
    ).reshape(4, -1)
    bias_grad = lax.dynamic_index_in_dim(vector_part[4], lane, axis=0, keepdims=True)
    vectors_grad = jnp.concatenate([norm_grad, bias_grad, bias_grad], axis=0)

    own_width = reduced[0].shape[2]
    own_bias = lax.dynamic_slice_in_dim(
        full_vectors[4] + full_vectors[5], lane * own_width, own_width, 0
    ).reshape(1, -1)
    layer_output, input_gradient = finish_rows(
        lens, layer_input, cotangent, jnp.concatenate(reduced, axis=1), own_bias, slots
    )

    results = [layer_output, input_gradient]
    for master, moments, grad in (
        (projector, projector_moments, projector_grad),
        (shifts, shifts_moments, shifts_grad),
        (combiner, combiner_moments, combiner_grad),
        (expander, expander_moments, expander_grad),
        (offsets, offsets_moments, offsets_grad),
        (reducer, reducer_moments, reducer_grad),
        (vectors, vectors_moments, vectors_grad),
    ):
        states, update = adamw(master, moments, grad)
        results += [grad, states, update]
    return tuple(results)


def solution(mesh):
    rows = P("dp", "tensor")
    cols = P("tensor", "dp")
    deep_rows = P(None, "dp", "tensor")
    deep_cols = P(None, "tensor", "dp")
    both = P(None, ("dp", "tensor"))
    deep_both = P(None, None, ("dp", "tensor"))
    placed = (P("dp", None), P("dp", None), P("dp"))
    results = (rows, rows)
    for plain, deep in (
        (rows, deep_rows),
        (cols, deep_cols),
        (cols, deep_cols),
        (rows, deep_rows),
        (cols, deep_cols),
        (cols, deep_cols),
        (both, deep_both),
    ):
        placed += (plain, deep)
        results += (plain, deep, plain)
    return jax.shard_map(
        on_device, mesh=mesh, in_specs=placed, out_specs=results, check_vma=False
    )
```

time: 1200 us -> 845 us (0.70)
  matrix products: 267 us -> 0 us
  Pallas kernels: 0 us -> 207 us
  waiting for transfers between devices: 565 us -> 445 us
  other arithmetic: 130 us -> 44.7 us
  local copies, waits for them, and re-layouts: 123 us -> 46.6 us
    dot_general x33 -> x0, matrix products: 267 us -> none  [the longest x4 76.4 us: contract_cols(): lax.dot_general(left, right, (((1,), (1,)), ((), ())), preferred_element_...]
    pallas_call x0 -> x10, Pallas kernels: none -> 207 us  [the longest x3 90.9 us: middle(): pl.pallas_call(kernel, out_shape=(hidden_shape, hidden_shape, jax.ShapeDt...]
    reduce_scatter x7 -> x6, waiting for transfers between devices: 506 us -> 402 us  [the longest x3 225 us: on_device(): lax.psum_scatter(both, 'tensor', scatter_dimension=2, tiled=True)]
    reduce_sum x8 -> x0, other arithmetic: 36.1 us -> none  [the longest x1 14.1 us: norm_layer(): return centred * lax.rsqrt(variance + layer_eps) * scale_row + shift_row]
    convert_element_type x12 -> x3, other arithmetic: 40.3 us -> 4.31 us  [the longest x1 2.72 us: on_device(): expand_own = expander.astype(BF16)]
    unnamed x17 -> x11, waiting for transfers between devices: 46.8 us -> 13.4 us
    convert_element_type x5 -> x1, local copies, waits for them, and re-layouts: 30.8 us -> 0.03 us  [on_device(): lax.all_gather(small, ('dp', 'tensor'), axis=0, tiled=True).astype(F32)]
    slice x10, local copies, waits for them, and re-layouts: 32.2 us -> 7.14 us  [the longest x2 2.61 us: on_device(): shifts_grad = packed[begin:begin + shifts.size].reshape(shifts.shape)]
  transfers between devices with their start and end apart: 14 -> 10, of which waited for: 9 -> 8; matrix products, arithmetic and copies ran while one was open for 35% -> 9% of each run, Pallas kernels for 0% -> 13%
where the time goes in v1:
time: 845 us; the launch traced here: 842 us
  waiting for transfers between devices  445 us (53%)
  Pallas kernels  207 us (24%)
  blocking collectives  82.9 us (10%)
  local copies, waits for them, and re-layouts  46.6 us (6%)
  other arithmetic  44.7 us (5%)
  between operations  14.8 us (2%)
    reduce_scatter x3, waiting for transfers between devices, on_device(): lax.psum_scatter(both, 'tensor', scatter_dimension=2, tiled=True)  225 us
    reduce_scatter x3, waiting for transfers between devices, reduce_pieces(): lax.psum_scatter(pieces[0], 'dp', scatter_dimension=0, tiled=True)[0]  176 us
    pallas_call x3, Pallas kernels, middle(): pl.pallas_call(kernel, out_shape=(hidden_shape, hidden_shape, jax.ShapeDt...  90.9 us
    all_gather x1, blocking collectives, on_device(): lax.all_gather(small, ('dp', 'tensor'), axis=0, tiled=True).astype(F32)  71.2 us
    pallas_call x3, Pallas kernels, gradient(): pl.pallas_call(kernel, out_shape=out_shape, grid_spec=pltpu.PrefetchScala...  49.3 us
    all_gather x3, waiting for transfers between devices, gather_weight(): lax.all_gather(own, 'dp', axis=0, tiled=True)  30.2 us
    unnamed x80, local copies, waits for them, and re-layouts  30 us
    pallas_call x1, Pallas kernels, attend(): pl.pallas_call(kernel, out_shape=(jax.ShapeDtypeStruct((rows, heads * HD)...  24.3 us
  transfers between devices with their start and end apart: 10, of which 8 were waited for; matrix products, arithmetic and copies ran while one was open for 9% of the time, Pallas kernels for 13%

profile of v1, /device:TPU:0, one launch (start us, length us, event | category | flops | bytes accessed | tf_op | source)
XLA Modules:
  0.0 842.1 jit_solution(15501064965444697495)
XLA Ops:
  7.2 1.3 copy.106
  8.8 1.1 pad_maximum_fusion.4
  10.0 1.9 copy.107
  12.0 1.2 convert_bitcast_fusion.2
  13.7 2.7 convert_element_type.45
  16.8 71.2 %all-gather = bf16[32768]{0:T(1024)(128)(2,1)S(1)} all-gather(bf16[1024]{0:T(1024)(128)(2,1)S(1)} %fusion.44), channel_id=2, replica_groups=mesh['dp'=8,'tensor'=4] {'dp','tensor'}, dimensions={0}, use_global_device_ids=true | all-gather | bytes 67584 | tf_op jit(solution)/shard_map/all_gather | solution.py:752
  91.3 15.3 %norm_rows.1 = (bf16[1536,2048]{1,0:T(8,128)(2,1)}, bf16[1536,2048]{1,0:T(8,128)(2,1)}, bf16[1536,2048]{1,0:T(8,128)(2,1)}, bf16[1536,2048]{1,0:T(8,128)(2,1)}) custom-call(s32[8]{0:T(128)} %pad_add_fusion.lens_ref, bf16[1536,2048]{1,0:T(8,128)(2,1)} %x_ref.3, bf16[1536,2048]{1,0:T(8,128)(2,1)} %cot_ref.3, f32[8,2048]{1,0:T(8,128)} %pad.14.vec_ref), custom_call_target="tpu_custom_call" | custom-call | flops 25165824 | bytes 37748736 | tf_op jit(solution)/shard_map/norm_rows/pallas_call | solution.py:143
  108.8 17.8 %project_rows.1 = (bf16[1536,1536]{1,0:T(8,128)(2,1)}, bf16[1536,512]{1,0:T(8,128)(2,1)}) custom-call(s32[8]{0:T(128)} %pad_add_fusion.lens_ref, bf16[1536,2048]{1,0:T(8,128)(2,1)} %get-tuple-element.48.n_ref.rest_0_, bf16[1536,2048]{1,0:T(8,128)(2,1)} %get-tuple-element.47.up_ref.rest_1_.rest_0_, f32[1,1536]{1,0:T(1,128)} %reshape.344.shift_ref, ...), custom_call_target="tpu_custom_call" | custom-call | flops 12884901888 | bytes 25165824 | tf_op jit(solution)/shard_map/project_rows/pallas_call | solution.py:231
  126.6 24.3 %attend.1 = (bf16[1536,512]{1,0:T(8,128)(2,1)}, bf16[1536,1536]{1,0:T(8,128)(2,1)}, f32[8,1536]{1,0:T(8,128)}) custom-call(s32[8]{0:T(128)} %pad_add_fusion.lens_ref, bf16[1536,1536]{1,0:T(8,128)(2,1)} %get-tuple-element.49.qkv_ref, bf16[1536,512]{1,0:T(8,128)(2,1)} %get-tuple-element.50.back_ref, f32[3,512,128]{2,1,0:T(8,128)} %pad_maximum_fusion.6.table_ref), custom_call_target="tpu_custom_call" | custom-call | flops 5637144576 | bytes 14155776 | tf_op jit(solution)/shard_map/attend/pallas_call | solution.py:357
  151.0 30.2 %all-gather.7.cloned.1.call-done.rest_1_ = bf16[2048,2048]{1,0:T(8,128)(2,1)} async-done(((bf16[256,2048]{1,0:T(8,128)(2,1)}), bf16[2048,2048]{1,0:T(8,128)(2,1)}) %all-gather.7.cloned.1.call-update) | async-done | bytes 8388624 | tf_op jit(solution)/shard_map/all_gather | solution.py:706
  181.2 24.7 %middle.3 = (bf16[1536,2048]{1,0:T(8,128)(2,1)}, bf16[1536,2048]{1,0:T(8,128)(2,1)}, bf16[2,256,2048]{2,1,0:T(8,128)(2,1)}, f32[8,2048]{1,0:T(8,128)}) custom-call(s32[8]{0:T(128)} %pad_add_fusion.lens_ref, bf16[1536,2048]{1,0:T(8,128)(2,1)} %get-tuple-element.46.n_ref.rest_0_, bf16[1536,2048]{1,0:T(8,128)(2,1)} %get-tuple-element.47.up_ref.rest_1_.rest_0_, ...), custom_call_target="tpu_custom_call" | custom-call | flops 10737418240 | bytes 33554432 | tf_op jit(solution)/shard_map/middle/pallas_call | solution.py:503
  205.9 39.5 %middle.4 = (bf16[1536,2048]{1,0:T(8,128)(2,1)}, bf16[1536,2048]{1,0:T(8,128)(2,1)}, bf16[2,512,2048]{2,1,0:T(8,128)(2,1)}, f32[8,2048]{1,0:T(8,128)}) custom-call(s32[8]{0:T(128)} %pad_add_fusion.lens_ref, bf16[1536,2048]{1,0:T(8,128)(2,1)} %get-tuple-element.46.n_ref.rest_0_, ...), custom_call_target="tpu_custom_call", output_to_operand_aliasing={{0}: (11, {}), {1}: (12, {})} | custom-call | flops 21474836480 | bytes 41943040 | tf_op jit(solution)/shard_map/middle/pallas_call | solution.py:503
  245.5 26.7 %middle.5 = (bf16[1536,2048]{1,0:T(8,128)(2,1)}, bf16[1536,2048]{1,0:T(8,128)(2,1)}, bf16[2,768,2048]{2,1,0:T(8,128)(2,1)}, f32[8,2048]{1,0:T(8,128)}) custom-call(s32[8]{0:T(128)} %pad_add_fusion.lens_ref, bf16[1536,2048]{1,0:T(8,128)(2,1)} %get-tuple-element.46.n_ref.rest_0_, ...), custom_call_target="tpu_custom_call", output_to_operand_aliasing={{0}: (11, {}), {1}: (12, {})} | custom-call | flops 32212254720 | bytes 50331648 | tf_op jit(solution)/shard_map/middle/pallas_call | solution.py:503
  274.8 16.2 %gradient.5 = bf16[8,256,2048]{2,1,0:T(8,128)(2,1)} custom-call(s32[8]{0:T(128)} %pad_add_fusion.lens_ref, bf16[1536,2048]{1,0:T(8,128)(2,1)} %get-tuple-element.47.up_ref.rest_1_.rest_0_, bf16[1536,2048]{1,0:T(8,128)(2,1)} %get-tuple-element.68.rest_1_), custom_call_target="tpu_custom_call" | custom-call | flops 12884901888 | bytes 20971520 | tf_op jit(solution)/shard_map/gradient/pallas_call | solution.py:613
  291.1 17.1 %gradient.3 = bf16[8,256,2048]{2,1,0:T(8,128)(2,1)} custom-call(s32[8]{0:T(128)} %pad_add_fusion.lens_ref, bf16[1536,2048]{1,0:T(8,128)(2,1)} %get-tuple-element.48.n_ref.rest_0_, bf16[1536,2048]{1,0:T(8,128)(2,1)} %get-tuple-element.47.up_ref.rest_1_.rest_0_, bf16[1536,1536]{1,0:T(8,128)(2,1)} %get-tuple-element.52.dp_ref.rest_2_, ...), custom_call_target="tpu_custom_call" | custom-call | flops 12884901888 | bytes 20971520 | tf_op jit(solution)/shard_map/gradient/pallas_call | solution.py:613
  308.2 16.0 %gradient.4 = bf16[8,256,2048]{2,1,0:T(8,128)(2,1)} custom-call(s32[8]{0:T(128)} %pad_add_fusion.lens_ref, bf16[1536,2048]{1,0:T(8,128)(2,1)} %get-tuple-element.46.n_ref.rest_0_, bf16[1536,2048]{1,0:T(8,128)(2,1)} %get-tuple-element.67.rest_1_), custom_call_target="tpu_custom_call" | custom-call | flops 12884901888 | bytes 20971520 | tf_op jit(solution)/shard_map/gradient/pallas_call | solution.py:613
  328.0 3.8 fusion.61
  331.8 2.9 copy.128
  334.7 1.8 copy.129
  336.6 1.4 fusion.62
  341.8 11.8 %all-reduce.7.cloned.1.call-done = f32[8,2048]{1,0:T(8,128)} async-done(((f32[8,2048]{1,0:T(8,128)}), f32[8,2048]{1,0:T(8,128)}) %all-reduce.7.cloned.1.call-update) | async-done | bytes 65552
  353.6 1.4 dynamic-slice_reduce_fusion
  355.2 11.7 %all-reduce.4 = f32[4,256]{1,0:T(4,128)S(1)} all-reduce(f32[4,256]{1,0:T(4,128)S(1)} %reshape.356), channel_id=10, replica_groups=mesh['dp'=8,'tensor'=4] {'tensor'}, use_global_device_ids=true, to_apply=%region_7.8.clone | all-reduce | flops 1024 | bytes 8192
  367.3 1.4 fusion.59
  368.8 1.5 dynamic-slice_reduce_fusion.1
  371.1 2.1 fusion.60
  376.4 51.4 %reduce-scatter.17.cloned.1.call-done = bf16[1,256,2048]{2,1,0:T(8,128)(2,1)} async-done(((bf16[8,256,2048]{2,1,0:T(8,128)(2,1)}), bf16[1,256,2048]{2,1,0:T(8,128)(2,1)}) %reduce-scatter.17.cloned.1.call-update) | async-done | bytes 1048592 | tf_op jit(solution)/shard_map/reduce_scatter | solution.py:710
  427.8 5.5 add_multiply_fusion
  433.3 2.3 pad_maximum_fusion.1
  435.6 6.2 copy.122
  441.8 1.8 copy.123
  443.9 1.8 copy.121
  445.7 57.0 %reduce-scatter.13.cloned.1.call-done = bf16[1,256,2048]{2,1,0:T(8,128)(2,1)} async-done(((bf16[8,256,2048]{2,1,0:T(8,128)(2,1)}), bf16[1,256,2048]{2,1,0:T(8,128)(2,1)}) %reduce-scatter.13.cloned.1.call-update) | async-done | bytes 1048592 | tf_op jit(solution)/shard_map/reduce_scatter | solution.py:710
  502.6 1.5 bitcast_convert_fusion
  504.2 1.2 add_multiply_fusion.2
  505.5 1.3 copy.119
  506.8 2.0 copy.120
  509.9 67.8 %reduce-scatter.15.cloned.1.call-done = bf16[1,256,2048]{2,1,0:T(8,128)(2,1)} async-done(((bf16[8,256,2048]{2,1,0:T(8,128)(2,1)}), bf16[1,256,2048]{2,1,0:T(8,128)(2,1)}) %reduce-scatter.15.cloned.1.call-update) | async-done | bytes 1048592 | tf_op jit(solution)/shard_map/reduce_scatter | solution.py:710
  577.6 3.6 fusion.10
  581.3 2.6 pad_maximum_fusion
  585.1 2.3 add_multiply_fusion.1
  588.6 1.9 pad_maximum_fusion.3
  590.5 33.6 %reduce-scatter.7.cloned.1.call-done = bf16[2,256,512]{2,1,0:T(8,128)(2,1)} async-done(((bf16[2,256,2048]{2,1,0:T(8,128)(2,1)}), bf16[2,256,512]{2,1,0:T(8,128)(2,1)}) %reduce-scatter.7.cloned.1.call-update) | async-done | bytes 524304 | tf_op jit(solution)/shard_map/reduce_scatter | solution.py:799
  624.1 78.3 %reduce-scatter.9.cloned.1.call-done = bf16[2,512,512]{2,1,0:T(8,128)(2,1)} async-done(((bf16[2,512,2048]{2,1,0:T(8,128)(2,1)}), bf16[2,512,512]{2,1,0:T(8,128)(2,1)}) %reduce-scatter.9.cloned.1.call-update) | async-done | bytes 1048592 | tf_op jit(solution)/shard_map/reduce_scatter | solution.py:799
  702.5 113.5 %reduce-scatter.11.cloned.1.call-done = bf16[2,768,512]{2,1,0:T(8,128)(2,1)} async-done(((bf16[2,768,2048]{2,1,0:T(8,128)(2,1)}), bf16[2,768,512]{2,1,0:T(8,128)(2,1)}) %reduce-scatter.11.cloned.1.call-update) | async-done | bytes 1572880 | tf_op jit(solution)/shard_map/reduce_scatter | solution.py:799
  816.0 3.7 pad_maximum_fusion.2.sum_ref
  819.6 9.7 %finish_rows.1 = (bf16[1536,512]{1,0:T(8,128)(2,1)}, bf16[1536,512]{1,0:T(8,128)(2,1)}) custom-call(s32[8]{0:T(128)} %pad_add_fusion.lens_ref, bf16[1536,2048]{1,0:T(8,128)(2,1)} %x_ref.3, bf16[1536,2048]{1,0:T(8,128)(2,1)} %cot_ref.3, bf16[2,1536,512]{2,1,0:T(8,128)(2,1)} %pad_maximum_fusion.2.sum_ref, f32[1,512]{1,0:T(1,128)} %bitcast.216), custom_call_target="tpu_custom_call" | custom-call | flops 3145728 | bytes 9437184 | tf_op jit(solution)/shard_map/finish_rows/pallas_call | solution.py:664
  829.3 5.8 fusion.12
  (161 shorter events, 25.4 us)
Async XLA Ops:
  7.2 1.6 copy-start.5
  7.2 101.6 %all-gather.5.cloned.1.call-start = ((), (), s32[]{:S(2)}) async-start(), calls=%async_computation.6 | async-start | bytes 9437184 | tf_op jit(solution)/shard_map/all_gather | solution.py:706
  8.6 1.3 copy-start.8
  10.0 141.0 %all-gather.9.cloned.1.call-start = ((), (), s32[]{:S(2)}) async-start(), calls=%async_computation.8 | async-start | bytes 9437184 | tf_op jit(solution)/shard_map/all_gather | solution.py:706
  12.0 1.7 copy-start
  13.6 2.9 copy-start.17
  13.6 3.0 copy-start.24
  13.6 3.1 copy-start.26
  13.6 77.0 %copy-start.28 = (s32[3]{0:T(128)S(1)}, s32[3]{0:T(128)}, u32[]{:S(2)}) copy-start(s32[3]{0:T(128)} %param.19) | copy-start | bytes 40
  13.6 167.6 %all-gather.7.cloned.1.call-start = ((), (), s32[]{:S(2)}) async-start(), calls=%async_computation.7 | async-start | bytes 9437184 | tf_op jit(solution)/shard_map/all_gather | solution.py:706
  16.4 337.1 %all-reduce.7.cloned.1.call-start = ((), (), s32[]{:S(2)}) async-start(), calls=%async_computation.15 | async-start | bytes 131072
  88.9 17.6 %copy-start.14 = (f32[32,6,64]{2,1,0:T(8,128)}, f32[32,6,64]{2,1,0:T(8,128)S(1)}, u32[]{:S(2)}) copy-start(f32[32,6,64]{2,1,0:T(8,128)S(1)} %reshape.340) | copy-start | bytes 147460
  245.4 26.7 %copy-start.15 = (f32[8,2048]{1,0:T(8,128)S(1)}, f32[8,2048]{1,0:T(8,128)}, u32[]{:S(2)}) copy-start(f32[8,2048]{1,0:T(8,128)} %get-tuple-element.63) | copy-start | bytes 196612
  245.5 26.7 %copy-start.16 = (f32[8,2048]{1,0:T(8,128)S(1)}, f32[8,2048]{1,0:T(8,128)}, u32[]{:S(2)}) copy-start(f32[8,2048]{1,0:T(8,128)} %get-tuple-element.64) | copy-start | bytes 196612
  274.8 153.0 %reduce-scatter.17.cloned.1.call-start = ((), (), s32[]{:S(2)}) async-start(), calls=%async_computation.14 | async-start | bytes 9437184 | tf_op jit(solution)/shard_map/reduce_scatter | solution.py:710
  291.0 211.6 %reduce-scatter.13.cloned.1.call-start = ((), (), s32[]{:S(2)}) async-start(), calls=%async_computation.12 | async-start | bytes 9437184 | tf_op jit(solution)/shard_map/reduce_scatter | solution.py:710
  308.2 269.4 %reduce-scatter.15.cloned.1.call-start = ((), (), s32[]{:S(2)}) async-start(), calls=%async_computation.13 | async-start | bytes 9437184 | tf_op jit(solution)/shard_map/reduce_scatter | solution.py:710
  324.3 299.9 %reduce-scatter.7.cloned.1.call-start = ((), (), s32[]{:S(2)}) async-start(), calls=%async_computation.9 | async-start | bytes 2621440 | tf_op jit(solution)/shard_map/reduce_scatter | solution.py:799
  325.0 377.5 %reduce-scatter.9.cloned.1.call-start = ((), (), s32[]{:S(2)}) async-start(), calls=%async_computation.10 | async-start | bytes 5242880 | tf_op jit(solution)/shard_map/reduce_scatter | solution.py:799
  325.8 490.2 %reduce-scatter.11.cloned.1.call-start = ((), (), s32[]{:S(2)}) async-start(), calls=%async_computation.11 | async-start | bytes 7864320 | tf_op jit(solution)/shard_map/reduce_scatter | solution.py:799
  326.2 0.7 copy-start.30
  326.2 1.2 copy-start.29
  336.5 5.2 copy-start.22
  336.5 36.8 %copy-start.21 = (f32[2,2,128]{2,1,0:T(2,128)S(1)}, f32[2,2,128]{2,1,0:T(2,128)}, u32[]{:S(2)}) copy-start(f32[2,2,128]{2,1,0:T(2,128)} %param.29) | copy-start | bytes 6148
  336.5 37.4 %copy-start.20 = (f32[2,2,96]{2,1,0:T(2,128)S(1)}, f32[2,2,96]{2,1,0:T(2,128)}, u32[]{:S(2)}) copy-start(f32[2,2,96]{2,1,0:T(2,128)} %param.23) | copy-start | bytes 4612
  336.5 38.0 %copy-start.25 = (f32[2,96]{1,0:T(2,128)S(1)}, f32[2,96]{1,0:T(2,128)}, u32[]{:S(2)}) copy-start(f32[2,96]{1,0:T(2,128)} %param.22) | copy-start | bytes 2308
  336.5 38.6 %copy-start.27 = (f32[2,128]{1,0:T(2,128)S(1)}, f32[2,128]{1,0:T(2,128)}, u32[]{:S(2)}) copy-start(f32[2,128]{1,0:T(2,128)} %param.28) | copy-start | bytes 3076
  336.6 39.2 %copy-start.18 = (f32[6,64]{1,0:T(8,128)S(1)}, f32[6,64]{1,0:T(8,128)}, u32[]{:S(2)}) copy-start(f32[6,64]{1,0:T(8,128)} %param.32) | copy-start | bytes 4612
  336.6 91.2 %copy-start.1 = (f32[2048,256]{0,1:T(8,128)S(1)}, f32[2048,256]{0,1:T(8,128)}, u32[]{:S(2)}) copy-start(f32[2048,256]{0,1:T(8,128)} %copy-done) | copy-start | bytes 6291460
  370.3 63.0 %copy-start.19 = (f32[1,256]{1,0:T(1,128)}, f32[1,256]{1,0:T(1,128)S(1)}, u32[]{:S(2)}) copy-start(f32[1,256]{1,0:T(1,128)S(1)} %get-tuple-element.188) | copy-start | bytes 3076
  373.4 60.0 %copy-start.23 = (f32[2,96]{1,0:T(2,128)}, f32[2,96]{1,0:T(2,128)S(1)}, u32[]{:S(2)}) copy-start(f32[2,96]{1,0:T(2,128)S(1)} %reshape.352) | copy-start | bytes 2308
  435.6 6.2 copy-start.4
  441.8 1.8 copy-start.11
  445.7 58.5 %copy-start.9 = (f32[512,256]{0,1:T(8,128)S(1)}, f32[512,256]{0,1:T(8,128)}, u32[]{:S(2)}) copy-start(f32[512,256]{0,1:T(8,128)} %copy-done.8) | copy-start | bytes 1572868
  445.7 58.5 %copy-start.12 = (f32[1,512,256]{1,2,0:T(8,128)S(1)}, f32[1,512,256]{1,2,0:T(8,128)}, u32[]{:S(2)}) copy-start(f32[1,512,256]{1,2,0:T(8,128)} %copy.126) | copy-start | bytes 1572868
  502.6 1.5 copy-start.13
  581.3 2.9 copy-start.2
  581.3 3.9 copy-start.6
  587.5 1.1 copy-start.7
  819.6 9.7 %copy-start.3 = (f32[256,2048]{1,0:T(8,128)S(1)}, f32[256,2048]{1,0:T(8,128)}, u32[]{:S(2)}) copy-start(f32[256,2048]{1,0:T(8,128)} %param.26) | copy-start | bytes 6291460
  819.6 9.7 %copy-start.10 = (bf16[1,256,2048]{2,1,0:T(8,128)(2,1)S(1)}, bf16[1,256,2048]{2,1,0:T(8,128)(2,1)}, u32[]{:S(2)}) copy-start(bf16[1,256,2048]{2,1,0:T(8,128)(2,1)} %reduce-scatter.15.cloned.1.call-done) | copy-start | bytes 3145732
Sparse Core Ops, SparseCore 0:
  10.5 57.1 all-gather.4
  70.1 54.2 all-gather.8
  126.9 54.2 all-gather.6
  274.9 78.6 all-reduce.6
  356.9 70.8 reduce-scatter.16
  431.1 71.4 reduce-scatter.12
  506.1 71.4 reduce-scatter.14
  580.5 43.5 reduce-scatter.6
  626.4 76.0 reduce-scatter.8
  704.6 111.2 reduce-scatter.10

commit v2 on v1

--- a/solution.py
+++ b/solution.py
@@ -29,8 +29,7 @@
 F32 = jnp.float32
 BF16 = jnp.bfloat16
 
-GATHER = "sc"
-REDUCE = "sc"
+MESH = pl.DeviceIdType.MESH
 
 
 def rotary_tables():
@@ -402,7 +401,7 @@
         refs = rest[:total]
         rest = rest[total + hold :]
         act_ref, dh_ref, both_ref, sum_ref = rest[:4]
-        held_e, held_x, held_s, done, dtwo, sems_e, sems_x, sems_s = rest[4:]
+        held_e, held_x, held_s, done, sems_e, sems_x, sems_s = rest[4:]
         i = pl.program_id(0)
 
         def fetch():
@@ -422,8 +421,6 @@
             for copy in fetch()[0]:
                 copy.wait()
             for copy in fetch()[1]:
-                copy.wait()
-            for copy in fetch()[2]:
                 copy.wait()
 
         @pl.when(first + i < live_blocks(lens_ref, slots))
@@ -441,6 +438,13 @@
                 dhidden = (dact * slope).astype(BF16)
                 dh_ref[:, cols] = dhidden
                 sum_ref[5:6, cols] += jnp.sum(dhidden.astype(F32), axis=0, keepdims=True)
+        @pl.when(i == 0)
+        def _():
+            for copy in fetch()[2]:
+                copy.wait()
+
+        @pl.when(first + i < live_blocks(lens_ref, slots))
+        def _():
             values = x_ref[...].astype(F32)
             centred, scale = norm_parts(values)
             hat = centred * scale
@@ -532,10 +536,6 @@
                 pltpu.VMEM((width, expand.width), BF16),
                 pltpu.VMEM((width, shrink.width), BF16),
                 pltpu.VMEM((BLOCK, width), F32),
-                pltpu.VMEM((8, 128), F32),
-            ]
-            + [pltpu.SemaphoreType.DMA((count,)) for count in (counts[1], counts[2], counts[0])][:0]
-            + [
                 pltpu.SemaphoreType.DMA((counts[0],)),
                 pltpu.SemaphoreType.DMA((counts[1],)),
                 pltpu.SemaphoreType.DMA((counts[2],)),
@@ -693,21 +693,172 @@
     return (jnp.stack([first_moment, root_moment]), update)
 
 
-def swap(values, mask, size):
+def exchange(values, spread, name, key):
+    dp, tensor = lax.axis_size("dp"), lax.axis_size("tensor")
+    count = dp * tensor
+    shape = values.shape if spread else values.shape[1:]
+
+    def kernel(x_ref, out_ref, send_sems, recv_sems):
+        me = lax.axis_index("dp") * tensor + lax.axis_index("tensor")
+        barrier = pltpu.get_barrier_semaphore()
+
+        def place(step):
+            other = lax.rem(me + step, count)
+            return other, (other // tensor, lax.rem(other, tensor))
+
+        @pl.loop(1, count)
+        def _(step):
+            _, target = place(step)
+            pl.semaphore_signal(barrier, inc=1, device_id=target, device_id_type=MESH)
+
+        pl.semaphore_wait(barrier, count - 1)
+
+        def copy(step):
+            other, target = place(step)
+            return pltpu.make_async_remote_copy(
+                src_ref=x_ref if spread else x_ref.at[other],
+                dst_ref=out_ref.at[me],
+                send_sem=send_sems.at[step],
+                recv_sem=recv_sems.at[step],
+                device_id=target,
+                device_id_type=MESH,
+            )
+
+        @pl.loop(1, count)
+        def _(step):
+            copy(step).start()
+
+        out_ref[me] = x_ref[...] if spread else x_ref[me]
+
+        @pl.loop(1, count)
+        def _(step):
+            copy(step).wait()
+
+    return pl.pallas_call(
+        kernel,
+        out_shape=jax.ShapeDtypeStruct((count, *shape), values.dtype),
+        in_specs=[pl.BlockSpec(memory_space=pltpu.VMEM)],
+        out_specs=pl.BlockSpec(memory_space=pltpu.VMEM),
+        scratch_shapes=[pltpu.SemaphoreType.DMA((count,)), pltpu.SemaphoreType.DMA((count,))],
+        compiler_params=pltpu.CompilerParams(collective_id=key, has_side_effects=True),
+        name=name,
+    )(values)
+
+
+def gather_cube(own, key):
+    shard, width = own.shape
+    parts = 4
+    step = shard // parts
+    orders = {2: (0, 1, 2, 3), 4: (2, 3, 0, 1)}
+
+    def kernel(own_ref, out_ref, keep_sem, send_sems, recv_sems):
+        me = lax.axis_index("dp")
+        barrier = pltpu.get_barrier_semaphore()
+        for mask in (1, 2, 4):
+            pl.semaphore_signal(
+                barrier, inc=1, device_id={"dp": me ^ mask}, device_id_type=MESH
+            )
+        pl.semaphore_wait(barrier, 3)
+
+        def rows(mask, part, count=1):
+            start = pl.multiple_of((me ^ mask) * shard + part * step, step)
+            return out_ref.at[pl.ds(start, count * step), :]
+
+        slot = iter(range(64))
+
+        def send(source, target, mask):
+            index = next(slot)
+            copy = pltpu.make_async_remote_copy(
+                src_ref=source,
+                dst_ref=target,
+                send_sem=send_sems.at[index],
+                recv_sem=recv_sems.at[index],
+                device_id={"dp": me ^ mask},
+                device_id_type=MESH,
+            )
+            copy.start()
+            return copy
+
+        keep = pltpu.make_async_copy(own_ref, rows(0, 0, parts), keep_sem)
+        first = {}
+        for turn_ in range(parts):
+            for mask in (2, 4):
+                part = orders[mask][turn_]
+                piece = own_ref.at[pl.ds(part * step, step), :]
+                first[mask, part] = send(piece, rows(0, part), mask)
+        late = [send(own_ref, rows(0, 0, parts), 1)]
+        keep.start()
+        second = []
+        for turn_ in range(parts):
+            for mask in (2, 4):
+                part = orders[mask][turn_]
+                first[mask, part].wait_recv()
+                piece = rows(mask, part)
+                late.append(send(piece, piece, 1))
+                if turn_ < parts // 2:
+                    second.append((6, part, send(piece, piece, 6 ^ mask)))
+        for mask, part, copy in second:
+            copy.wait_recv()
+            piece = rows(mask, part)
+            late.append(send(piece, piece, 1))
+        keep.wait()
+        for copy in late:
+            copy.wait()
+        for copy in first.values():
+            copy.wait_send()
+        for _, _, copy in second:
+            copy.wait_send()
+
+    sems = 64
+    return pl.pallas_call(
+        kernel,
+        out_shape=jax.ShapeDtypeStruct((8 * shard, width), own.dtype),
+        in_specs=[pl.BlockSpec(memory_space=pltpu.VMEM)],
+        out_specs=pl.BlockSpec(memory_space=pl.ANY),
+        scratch_shapes=[
+            pltpu.SemaphoreType.DMA,
+            pltpu.SemaphoreType.DMA((sems,)),
+            pltpu.SemaphoreType.DMA((sems,)),
+        ],
+        compiler_params=pltpu.CompilerParams(collective_id=key, has_side_effects=True),
+        name="gather_cube",
+    )(own)
+
+
+def swap(values, mask):
+    size = lax.axis_size("dp")
     return lax.ppermute(values, "dp", [(i, i ^ mask) for i in range(size)])
 
 
 def after(values, *others):
-    return lax.optimization_barrier((values, *others))[0]
-
-
-def gather_weight(own):
-    size = lax.axis_size("dp")
-    return Gathered([(lax.all_gather(own, "dp", axis=0, tiled=True), None, 0)], own.shape[0])
-
-
-def reduce_pieces(pieces):
-    return lax.psum_scatter(pieces[0], "dp", scatter_dimension=0, tiled=True)[0].astype(F32)
+    return lax.optimization_barrier((values, others))[0]
+
+
+def whole(full, shard):
+    return Gathered([(full, None, 0)], shard)
+
+
+def gather_plain(own):
+    return lax.all_gather(own, "dp", axis=0, tiled=True)
+
+
+def reduce_plain(parts):
+    return lax.psum_scatter(parts[0], "dp", scatter_dimension=0, tiled=True)[0].astype(F32)
+
+
+def reduce_cube(parts):
+    other, own = parts
+    half = own.shape[1] // 2
+    up = lambda v: v.astype(F32)
+    got = swap(other, 1)
+    send_x = (up(own[1::2, :half]) + up(got[1::2, :half])).astype(BF16)
+    send_y = (up(own[2:, half:]) + up(got[2:, half:])).astype(BF16)
+    from_x, from_y = swap(send_x, 2), swap(send_y, 4)
+    next_y = (up(own[2, :half]) + up(got[2, :half]) + up(from_x[1])).astype(BF16)
+    next_x = (up(own[1, half:]) + up(got[1, half:]) + up(from_y[1])).astype(BF16)
+    last_y, last_x = swap(next_y, 4), swap(next_x, 2)
+    mine = up(own[0]) + up(got[0])
+    return mine + jnp.concatenate([up(from_x[0]) + up(last_y), up(from_y[0]) + up(last_x)], axis=0)
 
 
 def on_device(
@@ -746,10 +897,12 @@
     expand_own = expander.astype(BF16)
     shrink_own = reducer.astype(BF16).T
 
+    cube = dp == 8
     sizes = [vectors.size, shifts.size, offsets.size]
     small = jnp.concatenate([vectors.reshape(-1), shifts.reshape(-1), offsets.reshape(-1)])
-    small = jnp.pad(small, (0, -small.size % 1024)).astype(BF16).reshape(1, -1)
-    small = lax.all_gather(small, ("dp", "tensor"), axis=0, tiled=True).astype(F32)
+    small = small.astype(BF16).astype(F32)
+    small = jnp.pad(small, (0, -small.size % 1024)).reshape(-1, 128)
+    small = exchange(small, True, "spread_small", 1).reshape(dp * tensor, -1)
     full_vectors = (
         small[:, : sizes[0]].reshape(dp * tensor, *vectors.shape).transpose(1, 0, 2).reshape(6, -1)
     )
@@ -770,27 +923,29 @@
     )
     vecs = jnp.pad(full_vectors, ((0, 2), (0, 0)))
 
-    entry = gather_weight(entry_own)
-    expand = gather_weight(expand_own)
-    shrink = gather_weight(shrink_own)
+    entry = whole(gather_cube(entry_own, 2) if cube else gather_plain(entry_own), shard)
+    expand = whole(gather_plain(expand_own), shard)
+    shrink = whole(gather_plain(shrink_own), shard)
+    reduce_parts = reduce_cube if cube else reduce_plain
 
     normed_one, normed_two, inputs, upstream = norm_rows(lens, layer_input, cotangent, vecs, slots)
     qkv, back = project_rows(
         lens, normed_one, upstream, entry, shift_row, table, slots, qkv_width
     )
     attended, dpacked, shift_sum = attend(lens, qkv, back, table, slots)
-    split = False
+    split = cube
     entry_parts = gradient(lens, [(normed_one, dpacked), (upstream, attended)], slots, shard, split)
 
     blocks = rows // BLOCK
     tensors = (normed_two, upstream, attended, dpacked, inputs)
+    mid_lens = after(lens, *entry_parts)
     carried = None
     sums = 0.0
     reduced = []
     first = 0
     for span in (1, 2, blocks - 3):
         act, dhid, both, part = middle(
-            lens, first, span, tensors, vecs, offset_row, entry, expand, shrink, carried, slots
+            mid_lens, first, span, tensors, vecs, offset_row, entry, expand, shrink, carried, slots
         )
         carried = (act, dhid)
         sums = sums + part
@@ -801,35 +956,42 @@
     shrink_parts = gradient(lens, [(upstream, act)], slots, shard, split)
     expand_parts = gradient(lens, [(normed_two, dhid)], slots, shard, split)
 
-    entry_share = reduce_pieces(entry_parts)
-    shrink_share = reduce_pieces(shrink_parts)
-    expand_share = reduce_pieces(expand_parts)
+    entry_share = reduce_parts(entry_parts)
+    shrink_share = reduce_parts(shrink_parts)
+    expand_share = reduce_parts(expand_parts)
     projector_grad = entry_share[:, :qkv_width]
     combiner_grad = entry_share[:, qkv_width:].T
     reducer_grad = shrink_share.T
     expander_grad = expand_share
 
-    shift_part = shift_sum[0].reshape(shifts.shape[0], dp, -1).transpose(1, 0, 2).reshape(dp, -1)
-    offset_part = (
-        sums[5, :hidden_width].reshape(offsets.shape[0], dp, -1).transpose(1, 0, 2).reshape(dp, -1)
-    )
-    vector_part = sums[:5, :width].reshape(5, dp, -1).transpose(1, 0, 2).reshape(dp, -1)
-    packed = jnp.concatenate([vector_part, shift_part, offset_part], axis=1)
-    used = packed.shape[1]
-    packed = jnp.pad(packed, ((0, 0), (0, -used % 1024)))
-    packed = lax.psum_scatter(packed, "dp", scatter_dimension=0, tiled=True)[0]
-    vector_part = packed[: vector_part.shape[1]].reshape(5, tensor, -1)
-    begin = vector_part.size
-    shifts_grad = packed[begin : begin + shifts.size].reshape(shifts.shape)
-    offsets_grad = packed[begin + shifts.size : used].reshape(offsets.shape)
-    norm_grad = lax.psum_scatter(
-        vector_part[:4].transpose(1, 0, 2).reshape(tensor, -1),
-        "tensor",
-        scatter_dimension=0,
-        tiled=True,
-    ).reshape(4, -1)
-    bias_grad = lax.dynamic_index_in_dim(vector_part[4], lane, axis=0, keepdims=True)
-    vectors_grad = jnp.concatenate([norm_grad, bias_grad, bias_grad], axis=0)
+    shift_part = shift_sum[0].reshape(shifts.shape[0], dp, -1).transpose(1, 0, 2).reshape(dp, 1, -1)
+    offset_part = sums[5, :hidden_width].reshape(offsets.shape[0], dp, -1)
+    offset_part = offset_part.transpose(1, 0, 2).reshape(dp, 1, -1)
+    norm_part = sums[:4, :width].reshape(4, dp, tensor, -1).transpose(1, 2, 0, 3)
+    bias_part = sums[4, :width].reshape(dp, tensor, -1)
+    alike = jnp.concatenate(
+        [
+            bias_part,
+            jnp.broadcast_to(shift_part, (dp, tensor, shifts.size)),
+            jnp.broadcast_to(offset_part, (dp, tensor, offsets.size)),
+        ],
+        axis=2,
+    )
+    alike = jnp.where(jnp.arange(tensor)[None, :, None] == lane, alike, 0.0)
+    packed = jnp.concatenate([norm_part.reshape(dp, tensor, -1), alike], axis=2)
+    used = packed.shape[2]
+    packed = jnp.pad(packed, ((0, 0), (0, 0), (0, -used % 1024)))
+    packed = exchange(packed.reshape(dp * tensor, -1, 128), False, "sum_small", 3)
+    packed = jnp.sum(packed, axis=0).reshape(-1)
+    marks = [4 * vectors.shape[1], vectors.shape[1], shifts.size, offsets.size]
+    marks = [sum(marks[:k]) for k in range(5)]
+    norm_grad, bias_grad, shifts_grad, offsets_grad = (
+        packed[low:high] for low, high in zip(marks, marks[1:])
+    )
+    shifts_grad = shifts_grad.reshape(shifts.shape)
+    offsets_grad = offsets_grad.reshape(offsets.shape)
+    bias_grad = bias_grad.reshape(1, -1)
+    vectors_grad = jnp.concatenate([norm_grad.reshape(4, -1), bias_grad, bias_grad], axis=0)
 
     own_width = reduced[0].shape[2]
     own_bias = lax.dynamic_slice_in_dim(

time: 845 us -> 524 us (0.62)
  waiting for transfers between devices: 445 us -> 49 us
  Pallas kernels: 207 us -> 335 us
  blocking collectives: 82.9 us -> 0 us
  other arithmetic: 44.7 us -> 68.5 us
  starting transfers between devices: 0.81 us -> 18.5 us
    reduce_scatter x3, waiting for transfers between devices: 225 us -> 0.02 us  [on_device(): lax.psum_scatter(both, 'tensor', scatter_dimension=2, tiled=True)]
    reduce_scatter x3 -> x0, waiting for transfers between devices: 176 us -> none  [reduce_pieces(): lax.psum_scatter(pieces[0], 'dp', scatter_dimension=0, tiled=True)[0]]
    pallas_call x0 -> x3, Pallas kernels: none -> 106 us  [the longest x1 64 us: gather_cube(): pl.pallas_call(kernel, out_shape=jax.ShapeDtypeStruct((8 * shard, width),...]
    all_gather x1 -> x0, blocking collectives: 71.2 us -> none  [on_device(): lax.all_gather(small, ('dp', 'tensor'), axis=0, tiled=True).astype(F32)]
    ppermute x0 -> x15, waiting for transfers between devices: none -> 48.9 us  [swap(): return lax.ppermute(values, 'dp', [(i, i ^ mask) for i in range(size)])]
    all_gather x3 -> x2, waiting for transfers between devices: 30.2 us -> 0.01 us  [gather_plain(): return lax.all_gather(own, 'dp', axis=0, tiled=True)]
    ppermute x0 -> x15, starting transfers between devices: none -> 18.1 us  [swap(): return lax.ppermute(values, 'dp', [(i, i ^ mask) for i in range(size)])]
    convert_element_type x1 -> x6, other arithmetic: 1.51 us -> 16.7 us  [the longest x3 8.79 us: reduce_cube(): send_x = (up(own[1::2, :half]) + up(got[1::2, :half])).astype(BF16)]
  transfers between devices with their start and end apart: 10 -> 20, of which waited for: 8 -> 7; matrix products, arithmetic and copies ran while one was open for 9% -> 19% of each run, Pallas kernels for 13% -> 62%
where the time goes in v2:
time: 524 us; the launch traced here: 527 us
  Pallas kernels  335 us (64%)
  other arithmetic  68.5 us (13%)
  waiting for transfers between devices  49 us (9%)
  local copies, waits for them, and re-layouts  42.1 us (8%)
  starting transfers between devices  18.5 us (4%)
  between operations  14.7 us (3%)
    pallas_call x3, Pallas kernels, middle(): pl.pallas_call(kernel, out_shape=(hidden_shape, hidden_shape, jax.ShapeDt...  97.4 us
    pallas_call x1, Pallas kernels, gather_cube(): pl.pallas_call(kernel, out_shape=jax.ShapeDtypeStruct((8 * shard, width),...  64 us
    pallas_call x3, Pallas kernels, gradient(): pl.pallas_call(kernel, out_shape=out_shape, grid_spec=pltpu.PrefetchScala...  56.6 us
    ppermute x15, waiting for transfers between devices, swap(): return lax.ppermute(values, 'dp', [(i, i ^ mask) for i in range(size)])  48.9 us
    pallas_call x2, Pallas kernels, exchange(): pl.pallas_call(kernel, out_shape=jax.ShapeDtypeStruct((count, *shape), va...  42.3 us
    unnamed x83, local copies, waits for them, and re-layouts  28.7 us
    pallas_call x1, Pallas kernels, attend(): pl.pallas_call(kernel, out_shape=(jax.ShapeDtypeStruct((rows, heads * HD)...  25.4 us
    pallas_call x1, Pallas kernels, project_rows(): pl.pallas_call(kernel, out_shape=(jax.ShapeDtypeStruct((rows, qkv_width),...  21.4 us
  transfers between devices with their start and end apart: 20, of which 7 were waited for; matrix products, arithmetic and copies ran while one was open for 19% of the time, Pallas kernels for 62%

profile of v2, /device:TPU:0, one launch (start us, length us, event | category | flops | bytes accessed | tf_op | source)
XLA Modules:
  0.0 527.4 jit_solution(475783819670323383)
XLA Ops:
  7.2 1.9 copy.65
  10.9 2.7 convert_element_type.266
  14.6 13.2 %spread_small.1 = f32[32,8,128]{2,1,0:T(8,128)} custom-call(f32[8,128]{1,0:T(8,128)} %fusion.52.x_ref), custom_call_target="tpu_custom_call" | custom-call | tf_op jit(solution)/shard_map/spread_small/pallas_call | solution.py:737
  32.9 64.0 %gather_cube.1.rest_0_ = bf16[2048,2048]{1,0:T(8,128)(2,1)} custom-call(bf16[256,2048]{1,0:T(8,128)(2,1)} %pad_maximum_fusion.4.own_ref), custom_call_target="tpu_custom_call" | custom-call | tf_op jit(solution)/shard_map/gather_cube/pallas_call | solution.py:813
  97.6 17.7 %norm_rows.1 = (bf16[1536,2048]{1,0:T(8,128)(2,1)}, bf16[1536,2048]{1,0:T(8,128)(2,1)}, bf16[1536,2048]{1,0:T(8,128)(2,1)}, bf16[1536,2048]{1,0:T(8,128)(2,1)}) custom-call(s32[8]{0:T(128)} %pad_add_fusion.lens_ref, bf16[1536,2048]{1,0:T(8,128)(2,1)} %x_ref.3, bf16[1536,2048]{1,0:T(8,128)(2,1)} %cot_ref.3, f32[8,2048]{1,0:T(8,128)} %pad.14.vec_ref), custom_call_target="tpu_custom_call" | custom-call | flops 25165824 | bytes 37748736 | tf_op jit(solution)/shard_map/norm_rows/pallas_call | solution.py:142
  117.6 21.4 %project_rows.1 = (bf16[1536,1536]{1,0:T(8,128)(2,1)}, bf16[1536,512]{1,0:T(8,128)(2,1)}) custom-call(s32[8]{0:T(128)} %pad_add_fusion.lens_ref, bf16[1536,2048]{1,0:T(8,128)(2,1)} %get-tuple-element.53.n_ref.rest_0_, bf16[1536,2048]{1,0:T(8,128)(2,1)} %get-tuple-element.54.up_ref.rest_1_.rest_0_, f32[1,1536]{1,0:T(1,128)} %reshape.376.shift_ref, ...), custom_call_target="tpu_custom_call" | custom-call | flops 12884901888 | bytes 25165824 | tf_op jit(solution)/shard_map/project_rows/pallas_call | solution.py:230
  139.0 25.4 %attend.1 = (bf16[1536,512]{1,0:T(8,128)(2,1)}, bf16[1536,1536]{1,0:T(8,128)(2,1)}, f32[8,1536]{1,0:T(8,128)}) custom-call(s32[8]{0:T(128)} %pad_add_fusion.lens_ref, bf16[1536,1536]{1,0:T(8,128)(2,1)} %get-tuple-element.55.qkv_ref, bf16[1536,512]{1,0:T(8,128)(2,1)} %get-tuple-element.56.back_ref, f32[3,512,128]{2,1,0:T(8,128)} %pad_maximum_fusion.6.table_ref), custom_call_target="tpu_custom_call" | custom-call | flops 5637144576 | bytes 14155776 | tf_op jit(solution)/shard_map/attend/pallas_call | solution.py:356
  164.4 19.2 %gradient.3 = (bf16[4,256,2048]{2,1,0:T(8,128)(2,1)}, bf16[4,256,2048]{2,1,0:T(8,128)(2,1)}) custom-call(s32[8]{0:T(128)} %pad_add_fusion.lens_ref, bf16[1536,2048]{1,0:T(8,128)(2,1)} %get-tuple-element.53.n_ref.rest_0_, bf16[1536,2048]{1,0:T(8,128)(2,1)} %get-tuple-element.54.up_ref.rest_1_.rest_0_, bf16[1536,1536]{1,0:T(8,128)(2,1)} %get-tuple-element.57.rest_2_.dp_ref, ...), custom_call_target="tpu_custom_call" | custom-call | flops 12884901888 | bytes 20971520 | tf_op jit(solution)/shard_map/gradient/pallas_call | solution.py:613
  184.4 22.5 %middle.3 = (bf16[1536,2048]{1,0:T(8,128)(2,1)}, bf16[1536,2048]{1,0:T(8,128)(2,1)}, bf16[2,256,2048]{2,1,0:T(8,128)(2,1)}, f32[8,2048]{1,0:T(8,128)}) custom-call(s32[8]{0:T(128)} %pad_add_fusion.lens_ref, bf16[1536,2048]{1,0:T(8,128)(2,1)} %get-tuple-element.62.n_ref.rest_0_, bf16[1536,2048]{1,0:T(8,128)(2,1)} %get-tuple-element.54.up_ref.rest_1_.rest_0_, ...), custom_call_target="tpu_custom_call" | custom-call | flops 10737418240 | bytes 33554432 | tf_op jit(solution)/shard_map/middle/pallas_call | solution.py:507
  207.6 3.0 add_convert_fusion.5
  210.6 10.7 %collective-permute-start.3 = (bf16[2,128,2048]{2,1,0:T(8,128)(2,1)S(1)}, bf16[2,128,2048]{2,1,0:T(8,128)(2,1)}, u32[]{:S(2)}, u32[]{:S(2)}) collective-permute-start(bf16[2,128,2048]{2,1,0:T(8,128)(2,1)S(1)} %get-tuple-element.152), channel_id=1, source_target_pairs={{0,16},{4,20},{8,24},{12,28},{16,0},{20,4},{24,8},{28,12},{1,17},{... | collective-permute-start | bytes 3145736 | tf_op jit(solution)/shard_map/ppermute | solution.py:830
  221.3 37.5 %middle.4 = (bf16[1536,2048]{1,0:T(8,128)(2,1)}, bf16[1536,2048]{1,0:T(8,128)(2,1)}, bf16[2,512,2048]{2,1,0:T(8,128)(2,1)}, f32[8,2048]{1,0:T(8,128)}) custom-call(s32[8]{0:T(128)} %pad_add_fusion.lens_ref, bf16[1536,2048]{1,0:T(8,128)(2,1)} %get-tuple-element.62.n_ref.rest_0_, ...), custom_call_target="tpu_custom_call", output_to_operand_aliasing={{0}: (11, {}), {1}: (12, {})} | custom-call | flops 21474836480 | bytes 41943040 | tf_op jit(solution)/shard_map/middle/pallas_call | solution.py:507
  259.1 4.5 fusion.67
  263.6 3.5 fusion.18
  270.0 1.9 copy.86
  271.9 2.9 copy.87
  276.1 2.0 copy.85
  278.8 1.9 collective-permute-done.2
  284.4 2.2 maximum_add_fusion
  288.0 1.8 copy-done.6
  289.8 2.8 add_multiply_fusion.1
  292.6 37.4 %middle.5 = (bf16[1536,2048]{1,0:T(8,128)(2,1)}, bf16[1536,2048]{1,0:T(8,128)(2,1)}, bf16[2,768,2048]{2,1,0:T(8,128)(2,1)}, f32[8,2048]{1,0:T(8,128)}) custom-call(s32[8]{0:T(128)} %pad_add_fusion.lens_ref, bf16[1536,2048]{1,0:T(8,128)(2,1)} %get-tuple-element.62.n_ref.rest_0_, ...), custom_call_target="tpu_custom_call", output_to_operand_aliasing={{0}: (11, {}), {1}: (12, {})} | custom-call | flops 32212254720 | bytes 50331648 | tf_op jit(solution)/shard_map/middle/pallas_call | solution.py:507
  330.0 18.6 %gradient.5 = (bf16[4,256,2048]{2,1,0:T(8,128)(2,1)}, bf16[4,256,2048]{2,1,0:T(8,128)(2,1)}) custom-call(s32[8]{0:T(128)} %pad_add_fusion.lens_ref, bf16[1536,2048]{1,0:T(8,128)(2,1)} %get-tuple-element.54.up_ref.rest_1_.rest_0_, bf16[1536,2048]{1,0:T(8,128)(2,1)} %get-tuple-element.80.rest_1_), custom_call_target="tpu_custom_call" | custom-call | flops 12884901888 | bytes 20971520 | tf_op jit(solution)/shard_map/gradient/pallas_call | solution.py:613
  348.6 18.9 %gradient.4 = (bf16[4,256,2048]{2,1,0:T(8,128)(2,1)}, bf16[4,256,2048]{2,1,0:T(8,128)(2,1)}) custom-call(s32[8]{0:T(128)} %pad_add_fusion.lens_ref, bf16[1536,2048]{1,0:T(8,128)(2,1)} %get-tuple-element.62.n_ref.rest_0_, bf16[1536,2048]{1,0:T(8,128)(2,1)} %get-tuple-element.77.rest_1_), custom_call_target="tpu_custom_call" | custom-call | flops 12884901888 | bytes 20971520 | tf_op jit(solution)/shard_map/gradient/pallas_call | solution.py:613
  369.9 2.1 copy.78
  374.2 3.1 fusion.24
  377.4 1.9 pad_maximum_fusion.3
  380.5 29.1 %sum_small.1 = f32[32,8,128]{2,1,0:T(8,128)} custom-call(f32[32,8,128]{2,1,0:T(8,128)} %reshape.382.x_ref), custom_call_target="tpu_custom_call" | custom-call | tf_op jit(solution)/shard_map/sum_small/pallas_call | solution.py:737
  412.8 3.3 add_convert_fusion.1
  416.2 1.6 collective-permute-start.11
  418.2 2.5 add_convert_fusion.3
  424.7 17.6 %collective-permute-done.11 = bf16[2,128,2048]{2,1,0:T(8,128)(2,1)S(1)} collective-permute-done((bf16[2,128,2048]{2,1,0:T(8,128)(2,1)S(1)}, bf16[2,128,2048]{2,1,0:T(8,128)(2,1)S(1)}, u32[]{:S(2)}, u32[]{:S(2)}) %collective-permute-start.11) | collective-permute-done | bytes 1048608 | tf_op jit(solution)/shard_map/ppermute | solution.py:830
  442.3 1.5 collective-permute-done.13
  443.8 1.7 fusion.22
  446.7 18.0 %collective-permute-done.6 = bf16[2,128,2048]{2,1,0:T(8,128)(2,1)S(1)} collective-permute-done((bf16[2,128,2048]{2,1,0:T(8,128)(2,1)S(1)}, bf16[2,128,2048]{2,1,0:T(8,128)(2,1)S(1)}, u32[]{:S(2)}, u32[]{:S(2)}) %collective-permute-start.6) | collective-permute-done | bytes 1048608 | tf_op jit(solution)/shard_map/ppermute | solution.py:830
  466.3 2.7 fusion.20
  470.1 7.4 %collective-permute-done.12 = bf16[128,2048]{1,0:T(8,128)(2,1)S(1)} collective-permute-done((bf16[128,2048]{1,0:T(8,128)(2,1)S(1)}, bf16[128,2048]{1,0:T(8,128)(2,1)S(1)}, u32[]{:S(2)}, u32[]{:S(2)}) %collective-permute-start.12) | collective-permute-done | bytes 524320 | tf_op jit(solution)/shard_map/ppermute | solution.py:830
  477.8 3.9 add_multiply_fusion
  483.1 2.5 pad_maximum_fusion.1
  485.6 1.8 copy.79
  487.4 5.5 %copy.80 = f32[2,2048,256]{2,1,0:T(8,128)} copy(f32[2,2048,256]{1,2,0:T(8,128)} %pad_maximum_fusion.1) | data formatting | bytes 8388608
  492.9 1.8 copy.81
  494.7 1.6 fusion.64
  497.6 2.9 multiply_add_fusion
  500.5 2.3 pad_maximum_fusion
  502.9 4.4 fusion.12
  507.4 3.7 pad_maximum_fusion.2.sum_ref
  511.1 9.6 %finish_rows.1 = (bf16[1536,512]{1,0:T(8,128)(2,1)}, bf16[1536,512]{1,0:T(8,128)(2,1)}) custom-call(s32[8]{0:T(128)} %pad_add_fusion.lens_ref, bf16[1536,2048]{1,0:T(8,128)(2,1)} %x_ref.3, bf16[1536,2048]{1,0:T(8,128)(2,1)} %cot_ref.3, bf16[2,1536,512]{2,1,0:T(8,128)(2,1)} %pad_maximum_fusion.2.sum_ref, f32[1,512]{1,0:T(1,128)} %bitcast.248), custom_call_target="tpu_custom_call" | custom-call | flops 3145728 | bytes 9437184 | tf_op jit(solution)/shard_map/finish_rows/pallas_call | solution.py:664
  (192 shorter events, 42.5 us)
Async XLA Ops:
  7.2 177.2 %all-gather.5.cloned.1.call-start = ((), (), s32[]{:S(2)}) async-start(), calls=%async_computation.4 | async-start | bytes 9437184 | tf_op jit(solution)/shard_map/all_gather | solution.py:842
  10.8 2.8 copy-start.22
  10.8 2.9 copy-start.29
  10.8 3.0 copy-start.31
  10.8 173.5 %all-gather.3.cloned.1.call-start = ((), (), s32[]{:S(2)}) async-start(), calls=%async_computation.3 | async-start | bytes 9437184 | tf_op jit(solution)/shard_map/all_gather | solution.py:842
  13.6 17.9 %copy-start.18 = (f32[512,256]{1,0:T(8,128)S(1)}, f32[512,256]{1,0:T(8,128)}, u32[]{:S(2)}) copy-start(f32[512,256]{1,0:T(8,128)} %param.24) | copy-start | bytes 1572868
  13.6 18.1 %copy-start.11 = (f32[256,1536]{1,0:T(8,128)S(1)}, f32[256,1536]{1,0:T(8,128)}, u32[]{:S(2)}) copy-start(f32[256,1536]{1,0:T(8,128)} %param.20) | copy-start | bytes 4718596
  13.6 493.7 %reduce-scatter.4.cloned.1.call-start = ((), (), s32[]{:S(2)}) async-start(), calls=%async_computation.5 | async-start | bytes 2621440 | tf_op jit(solution)/shard_map/reduce_scatter | solution.py:954
  32.9 64.0 %copy-start.33 = (s32[3]{0:T(128)S(1)}, s32[3]{0:T(128)}, u32[]{:S(2)}) copy-start(s32[3]{0:T(128)} %param.19) | copy-start | bytes 40
  183.6 24.0 %collective-permute-start = (bf16[4,256,2048]{2,1,0:T(8,128)(2,1)}, bf16[4,256,2048]{2,1,0:T(8,128)(2,1)}, u32[]{:S(2)}, u32[]{:S(2)}) collective-permute-start(bf16[4,256,2048]{2,1,0:T(8,128)(2,1)} %get-tuple-element.59), channel_id=1, source_target_pairs={{0,4},{4,0},{8,12},{12,8},{16,20},{20,16},{24,28},{28,24},{1,5},{5... | collective-permute-start | bytes 12582920 | tf_op jit(solution)/shard_map/ppermute | solution.py:830
  206.9 300.4 %reduce-scatter.6.cloned.1.call-start = ((), (), s32[]{:S(2)}) async-start(), calls=%async_computation.6 | async-start | bytes 5242880 | tf_op jit(solution)/shard_map/reduce_scatter | solution.py:954
  210.6 53.0 %collective-permute-start.1 = (bf16[2,128,2048]{2,1,0:T(8,128)(2,1)S(1)}, bf16[2,128,2048]{2,1,0:T(8,128)(2,1)}, u32[]{:S(2)}, u32[]{:S(2)}) collective-permute-start(bf16[2,128,2048]{2,1,0:T(8,128)(2,1)S(1)} %get-tuple-element.151), channel_id=1, source_target_pairs={{0,8},{4,12},{8,0},{12,4},{16,24},{20,28},{24,16},{28,20},{1,9},{5... | collective-permute-start | bytes 3145736 | tf_op jit(solution)/shard_map/ppermute | solution.py:830
  210.6 53.0 %collective-permute-start.3 = (bf16[2,128,2048]{2,1,0:T(8,128)(2,1)S(1)}, bf16[2,128,2048]{2,1,0:T(8,128)(2,1)}, u32[]{:S(2)}, u32[]{:S(2)}) collective-permute-start(bf16[2,128,2048]{2,1,0:T(8,128)(2,1)S(1)} %get-tuple-element.152), channel_id=1, source_target_pairs={{0,16},{4,20},{8,24},{12,28},{16,0},{20,4},{24,8},{28,12},{1,17},{... | collective-permute-start | bytes 3145736 | tf_op jit(solution)/shard_map/ppermute | solution.py:830
  258.9 248.5 %reduce-scatter.8.cloned.1.call-start = ((), (), s32[]{:S(2)}) async-start(), calls=%async_computation.7 | async-start | bytes 7864320 | tf_op jit(solution)/shard_map/reduce_scatter | solution.py:954
  263.6 4.7 copy-start.16
  267.1 13.6 %collective-permute-start.2 = (bf16[128,2048]{1,0:T(8,128)(2,1)}, bf16[128,2048]{1,0:T(8,128)(2,1)}, u32[]{:S(2)}, u32[]{:S(2)}) collective-permute-start(bf16[128,2048]{1,0:T(8,128)(2,1)} %get-tuple-element.149), channel_id=1, source_target_pairs={{0,16},{4,20},{8,24},{12,28},{16,0},{20,4},{24,8},{28,12},{1,17},{... | collective-permute-start | bytes 1572872 | tf_op jit(solution)/shard_map/ppermute | solution.py:830
  269.3 13.7 %collective-permute-start.4 = (bf16[128,2048]{1,0:T(8,128)(2,1)}, bf16[128,2048]{1,0:T(8,128)(2,1)}, u32[]{:S(2)}, u32[]{:S(2)}) collective-permute-start(bf16[128,2048]{1,0:T(8,128)(2,1)} %get-tuple-element.150), channel_id=1, source_target_pairs={{0,8},{4,12},{8,0},{12,4},{16,24},{20,28},{24,16},{28,20},{1,9},{5... | collective-permute-start | bytes 1572872 | tf_op jit(solution)/shard_map/ppermute | solution.py:830
  284.4 2.2 copy-start.14
  284.4 3.6 copy-start.12
  286.6 6.0 %copy-start.7 = (f32[256,2048]{1,0:T(8,128)}, f32[256,2048]{1,0:T(8,128)S(1)}, u32[]{:S(2)}) copy-start(f32[256,2048]{1,0:T(8,128)S(1)} %maximum_add_fusion) | copy-start | bytes 6291460
  286.6 3.2 copy-start.6
  348.6 64.2 %collective-permute-start.10 = (bf16[4,256,2048]{2,1,0:T(8,128)(2,1)}, bf16[4,256,2048]{2,1,0:T(8,128)(2,1)}, u32[]{:S(2)}, u32[]{:S(2)}) collective-permute-start(bf16[4,256,2048]{2,1,0:T(8,128)(2,1)} %get-tuple-element.82), channel_id=1, source_target_pairs={{0,4},{4,0},{8,12},{12,8},{16,20},{20,16},{24,28},{28,24},{1,5},{5... | collective-permute-start | bytes 12582920 | tf_op jit(solution)/shard_map/ppermute | solution.py:830
  348.6 18.9 %copy-start.15 = (f32[1,512,256]{1,2,0:T(8,128)S(1)}, f32[1,512,256]{1,2,0:T(8,128)}, u32[]{:S(2)}) copy-start(f32[1,512,256]{1,2,0:T(8,128)} %get-tuple-element.158) | copy-start | bytes 1572868
  367.5 50.6 %collective-permute-start.5 = (bf16[4,256,2048]{2,1,0:T(8,128)(2,1)}, bf16[4,256,2048]{2,1,0:T(8,128)(2,1)}, u32[]{:S(2)}, u32[]{:S(2)}) collective-permute-start(bf16[4,256,2048]{2,1,0:T(8,128)(2,1)} %get-tuple-element.79), channel_id=1, source_target_pairs={{0,4},{4,0},{8,12},{12,8},{16,20},{20,16},{24,28},{28,24},{1,5},{5... | collective-permute-start | bytes 12582920 | tf_op jit(solution)/shard_map/ppermute | solution.py:830
  377.3 33.2 %copy-start.25 = (f32[2,2,128]{2,1,0:T(2,128)S(1)}, f32[2,2,128]{2,1,0:T(2,128)}, u32[]{:S(2)}) copy-start(f32[2,2,128]{2,1,0:T(2,128)} %param.29) | copy-start | bytes 6148
  377.3 33.2 %copy-start.32 = (f32[2,128]{1,0:T(2,128)S(1)}, f32[2,128]{1,0:T(2,128)}, u32[]{:S(2)}) copy-start(f32[2,128]{1,0:T(2,128)} %param.28) | copy-start | bytes 3076
  377.3 35.5 %copy-start.24 = (f32[2,2,96]{2,1,0:T(2,128)S(1)}, f32[2,2,96]{2,1,0:T(2,128)}, u32[]{:S(2)}) copy-start(f32[2,2,96]{2,1,0:T(2,128)} %param.23) | copy-start | bytes 4612
  411.2 5.0 copy-start.28
  411.6 11.9 %copy-start.27 = (f32[2,96]{1,0:T(2,128)}, f32[2,96]{1,0:T(2,128)S(1)}, u32[]{:S(2)}) copy-start(f32[2,96]{1,0:T(2,128)S(1)} %reshape.384) | copy-start | bytes 2308
  412.8 5.3 %copy-start.10 = (bf16[4,256,2048]{2,1,0:T(8,128)(2,1)S(1)}, bf16[4,256,2048]{2,1,0:T(8,128)(2,1)}, u32[]{:S(2)}) copy-start(bf16[4,256,2048]{2,1,0:T(8,128)(2,1)} %get-tuple-element.78) | copy-start | bytes 12582916
  416.2 26.1 %collective-permute-start.11 = (bf16[2,128,2048]{2,1,0:T(8,128)(2,1)S(1)}, bf16[2,128,2048]{2,1,0:T(8,128)(2,1)S(1)}, u32[]{:S(2)}, u32[]{:S(2)}) collective-permute-start(bf16[2,128,2048]{2,1,0:T(8,128)(2,1)S(1)} %get-tuple-element.143), channel_id=1, source_target_pairs={{0,8},{4,12},{8,0},{12,4},{16,24},{20,28},{24,16},{28,20},{1,9},{5... | collective-permute-start | bytes 3145736 | tf_op jit(solution)/shard_map/ppermute | solution.py:830
  417.8 26.0 %collective-permute-start.13 = (bf16[2,128,2048]{2,1,0:T(8,128)(2,1)S(1)}, bf16[2,128,2048]{2,1,0:T(8,128)(2,1)S(1)}, u32[]{:S(2)}, u32[]{:S(2)}) collective-permute-start(bf16[2,128,2048]{2,1,0:T(8,128)(2,1)S(1)} %get-tuple-element.144), channel_id=1, source_target_pairs={{0,16},{4,20},{8,24},{12,28},{16,0},{20,4},{24,8},{28,12},{1,17},{... | collective-permute-start | bytes 3145736 | tf_op jit(solution)/shard_map/ppermute | solution.py:830
  418.2 5.3 %copy-start.30 = (f32[2,96]{1,0:T(2,128)S(1)}, f32[2,96]{1,0:T(2,128)}, u32[]{:S(2)}) copy-start(f32[2,96]{1,0:T(2,128)} %param.22) | copy-start | bytes 2308
  418.2 5.9 %copy-start.23 = (f32[6,64]{1,0:T(8,128)S(1)}, f32[6,64]{1,0:T(8,128)}, u32[]{:S(2)}) copy-start(f32[6,64]{1,0:T(8,128)} %param.32) | copy-start | bytes 4612
  418.2 25.6 %copy-start.13 = (bf16[4,256,2048]{2,1,0:T(8,128)(2,1)S(1)}, bf16[4,256,2048]{2,1,0:T(8,128)(2,1)}, u32[]{:S(2)}) copy-start(bf16[4,256,2048]{2,1,0:T(8,128)(2,1)} %get-tuple-element.81) | copy-start | bytes 12582916
  420.7 44.1 %collective-permute-start.6 = (bf16[2,128,2048]{2,1,0:T(8,128)(2,1)S(1)}, bf16[2,128,2048]{2,1,0:T(8,128)(2,1)S(1)}, u32[]{:S(2)}, u32[]{:S(2)}) collective-permute-start(bf16[2,128,2048]{2,1,0:T(8,128)(2,1)S(1)} %get-tuple-element.147), channel_id=1, source_target_pairs={{0,8},{4,12},{8,0},{12,4},{16,24},{20,28},{24,16},{28,20},{1,9},{5... | collective-permute-start | bytes 3145736 | tf_op jit(solution)/shard_map/ppermute | solution.py:830
  421.5 44.8 %collective-permute-start.8 = (bf16[2,128,2048]{2,1,0:T(8,128)(2,1)S(1)}, bf16[2,128,2048]{2,1,0:T(8,128)(2,1)S(1)}, u32[]{:S(2)}, u32[]{:S(2)}) collective-permute-start(bf16[2,128,2048]{2,1,0:T(8,128)(2,1)S(1)} %get-tuple-element.148), channel_id=1, source_target_pairs={{0,16},{4,20},{8,24},{12,28},{16,0},{20,4},{24,8},{28,12},{1,17},{... | collective-permute-start | bytes 3145736 | tf_op jit(solution)/shard_map/ppermute | solution.py:830
  445.5 32.0 %collective-permute-start.12 = (bf16[128,2048]{1,0:T(8,128)(2,1)S(1)}, bf16[128,2048]{1,0:T(8,128)(2,1)S(1)}, u32[]{:S(2)}, u32[]{:S(2)}) collective-permute-start(bf16[128,2048]{1,0:T(8,128)(2,1)S(1)} %get-tuple-element.141), channel_id=1, source_target_pairs={{0,16},{4,20},{8,24},{12,28},{16,0},{20,4},{24,8},{28,12},{1,17},{... | collective-permute-start | bytes 1572872 | tf_op jit(solution)/shard_map/ppermute | solution.py:830
  446.0 31.7 %collective-permute-start.14 = (bf16[128,2048]{1,0:T(8,128)(2,1)S(1)}, bf16[128,2048]{1,0:T(8,128)(2,1)S(1)}, u32[]{:S(2)}, u32[]{:S(2)}) collective-permute-start(bf16[128,2048]{1,0:T(8,128)(2,1)S(1)} %get-tuple-element.142), channel_id=1, source_target_pairs={{0,8},{4,12},{8,0},{12,4},{16,24},{20,28},{24,16},{28,20},{1,9},{5... | collective-permute-start | bytes 1572872 | tf_op jit(solution)/shard_map/ppermute | solution.py:830
  464.8 4.2 copy-start.17
  469.0 25.7 %collective-permute-start.7 = (bf16[128,2048]{1,0:T(8,128)(2,1)}, bf16[128,2048]{1,0:T(8,128)(2,1)}, u32[]{:S(2)}, u32[]{:S(2)}) collective-permute-start(bf16[128,2048]{1,0:T(8,128)(2,1)} %get-tuple-element.145), channel_id=1, source_target_pairs={{0,16},{4,20},{8,24},{12,28},{16,0},{20,4},{24,8},{28,12},{1,17},{... | collective-permute-start | bytes 1572872 | tf_op jit(solution)/shard_map/ppermute | solution.py:830
  469.3 8.4 %copy-start = (f32[1,2048,256]{1,2,0:T(8,128)S(1)}, f32[1,2048,256]{1,2,0:T(8,128)}, u32[]{:S(2)}) copy-start(f32[1,2048,256]{1,2,0:T(8,128)} %copy.87) | copy-start | bytes 6291460
  469.4 8.4 %copy-start.4 = (f32[2048,256]{0,1:T(8,128)S(1)}, f32[2048,256]{0,1:T(8,128)}, u32[]{:S(2)}) copy-start(f32[2048,256]{0,1:T(8,128)} %copy-done.3) | copy-start | bytes 6291460
  469.4 26.9 %collective-permute-start.9 = (bf16[128,2048]{1,0:T(8,128)(2,1)}, bf16[128,2048]{1,0:T(8,128)(2,1)}, u32[]{:S(2)}, u32[]{:S(2)}) collective-permute-start(bf16[128,2048]{1,0:T(8,128)(2,1)} %get-tuple-element.146), channel_id=1, source_target_pairs={{0,8},{4,12},{8,0},{12,4},{16,24},{20,28},{24,16},{28,20},{1,9},{5... | collective-permute-start | bytes 1572872 | tf_op jit(solution)/shard_map/ppermute | solution.py:830
  483.1 2.5 copy-start.2
  487.4 5.5 %copy-start.9 = (f32[2048,256]{0,1:T(8,128)S(1)}, f32[2048,256]{0,1:T(8,128)}, u32[]{:S(2)}) copy-start(f32[2048,256]{0,1:T(8,128)} %get-tuple-element.131) | copy-start | bytes 6291460
  494.7 2.9 copy-start.5
  500.5 2.4 copy-start.8
  (6 other events, 9.5 us)
Sparse Core Ops, SparseCore 0:
  10.6 80.3 all-gather.4
  93.4 54.3 all-gather.2
  207.0 51.8 reduce-scatter.3
  261.0 75.9 reduce-scatter.5
  348.7 127.3 reduce-scatter.7
